TPU v7x, 16 devices: a whole 2x2x2 slice. The times are simulated.
16 devices in a mesh: depth: 2 (over z), col: 2 (over y), row: 4 (over x, core).
Axes of the slice: x: 2, y: 2, z: 2, core: 2. Of those that a mesh axis runs over, the one named last changes fastest.
Arguments:
- tokens: bfloat16 [32768, 1280], P(('depth', 'row'), 'col')
- w_up: bfloat16 [1280, 5120], P('row', 'col')
- w_down: bfloat16 [5120, 1280], P('row', 'col')
- grad_out: bfloat16 [32768, 1280], P(('depth', 'row'), 'col')
Outputs:
- output 1: bfloat16 [32768, 1280], P(('depth', 'row'), 'col')
- output 2: bfloat16 [32768, 1280], P(('depth', 'row'), 'col')
- output 3: float32 [1280, 5120], P('row', 'col')
- output 4: float32 [5120, 1280], P('row', 'col')
All inputs are finite; a program needn't handle non-finite values.
Results may differ from a plain program's by a relative error of at most 0.001.
Values are sent between devices in bfloat16 or wider.
A program may use at most 1 GiB of HBM per device.

v0:
```python
import jax
import jax.numpy as jnp
from jax import lax
from jax.sharding import PartitionSpec as P


def gelu_fn(pre_act):
    return jax.nn.gelu(pre_act, approximate=True)


def solution(mesh):
    act_spec = P(("depth", "row"), "col")
    weight_spec = P("row", "col")
    contract_last = (((1,), (1,)), ((), ()))
    contract_first = (((0,), (0,)), ((), ()))

    def local_block(tok_blk, up_blk, down_blk, grad_blk):
        tok_full = lax.all_gather(tok_blk, "col", axis=1, tiled=True)
        up_cols = lax.all_gather(up_blk, "row", axis=0, tiled=True)
        down_cols = lax.all_gather(down_blk, "row", axis=0, tiled=True)
        pre_act = jnp.dot(tok_full, up_cols, preferred_element_type=jnp.float32)
        hidden, gelu_vjp = jax.vjp(gelu_fn, pre_act)
        hidden = hidden.astype(jnp.bfloat16)
        hidden_full = lax.all_gather(hidden, "col", axis=1, tiled=True)
        out_blk = jnp.dot(hidden_full, down_cols, preferred_element_type=jnp.float32).astype(jnp.bfloat16)
        d_hidden_part = lax.dot_general(grad_blk, down_cols, contract_last, preferred_element_type=jnp.float32)
        d_hidden = lax.psum_scatter(d_hidden_part, "col", scatter_dimension=1, tiled=True)
        d_pre = gelu_vjp(d_hidden)[0].astype(jnp.bfloat16)
        dx_part = lax.dot_general(d_pre, up_cols, contract_last, preferred_element_type=jnp.float32)
        dx_blk = lax.psum_scatter(dx_part, "col", scatter_dimension=1, tiled=True).astype(jnp.bfloat16)
        dw_up_part = lax.dot_general(tok_full, d_pre, contract_first, preferred_element_type=jnp.float32)
        dw_up_layer = lax.psum_scatter(dw_up_part, "row", scatter_dimension=0, tiled=True)
        dw_up = lax.psum(dw_up_layer, "depth")
        dw_down_part = lax.dot_general(hidden_full, grad_blk, contract_first, preferred_element_type=jnp.float32)
        dw_down_layer = lax.psum_scatter(dw_down_part, "row", scatter_dimension=0, tiled=True)
        dw_down = lax.psum(dw_down_layer, "depth")
        return out_blk, dx_blk, dw_up, dw_down

    return jax.shard_map(local_block, mesh=mesh, in_specs=(act_spec, weight_spec, weight_spec, act_spec), out_specs=(act_spec, act_spec, weight_spec, weight_spec), check_vma=False)
```

profile of v0, /device:TPU:0, one launch (start us, length us, event | category | flops | bytes accessed | tf_op | source)
XLA Modules:
  0.0 2311.7 jit_solution(9452644842310412064)
XLA Ops:
  7.2 0.0 all-gather.11.cloned.1.call-start
  7.2 0.7 all-gather.11.cloned.1.call-update
  7.9 0.0 all-gather.7.cloned.1.call-start
  7.9 0.7 all-gather.7.cloned.1.call-update
  8.6 0.0 all-gather.5.cloned.1.call-start
  8.7 0.7 all-gather.5.cloned.1.call-update
  9.4 0.0 reduce-scatter.7.cloned.1.call-start
  9.4 49.0 %all-gather.11.cloned.1.call-done = bf16[5120,640]{1,0:T(8,128)(2,1)} async-done(((bf16[1280,640]{1,0:T(8,128)(2,1)}), bf16[5120,640]{1,0:T(8,128)(2,1)}) %all-gather.11.cloned.1.call-update) | async-done | bytes 6553616 | tf_op jit(solution)/shard_map/all_gather | solution.py:20
  58.4 43.8 %fusion.7 = f32[4096,5120]{1,0:T(8,128)} fusion(bf16[4096,640]{1,0:T(8,128)(2,1)} %param.7, bf16[5120,640]{1,0:T(8,128)(2,1)} %all-gather.11.cloned.1.call-done), kind=kOutput, calls=%fused_computation.12 | convolution fusion | flops 26843545600 | bytes 95682560 | tf_op jit(solution)/shard_map/dot_general | solution.py:26
  102.2 0.0 reduce-scatter.7.cloned.1.call-update
  102.2 0.3 all-gather.9.cloned.1.call-start
  102.6 3.5 all-gather.7.cloned.1.call-done
  106.0 130.0 %all-gather.5.cloned.1.call-done = bf16[4096,1280]{1,0:T(8,128)(2,1)} async-done(((bf16[4096,640]{1,0:T(8,128)(2,1)}), bf16[4096,1280]{1,0:T(8,128)(2,1)}) %all-gather.5.cloned.1.call-update) | async-done | bytes 10485776 | tf_op jit(solution)/shard_map/all_gather | solution.py:18
  236.0 908.6 %reduce-scatter.7.cloned.1.call-done = f32[4096,2560]{1,0:T(8,128)} async-done(((f32[4096,5120]{1,0:T(8,128)}), f32[4096,2560]{1,0:T(8,128)}) %reduce-scatter.7.cloned.1.call-update) | async-done | bytes 41943056 | tf_op jit(solution)/shard_map/reduce_scatter | solution.py:27
  1144.7 65.5 %fusion.6 = (bf16[4096,2560]{1,0:T(8,128)(2,1)}, bf16[4096,2560]{1,0:T(8,128)(2,1)}) fusion(f32[4096,2560]{1,0:T(8,128)} %reduce-scatter.7.cloned.1.call-done, bf16[4096,1280]{1,0:T(8,128)(2,1)} %all-gather.5.cloned.1.call-done, bf16[1280,2560]{1,0:T(8,128)(2,1)} %all-gather.7.cloned.1.call-done), kind=kOutput, calls=%fused_computation.8 | convolution fusion | flops 27074232320 | bytes 100925440 | tf_op jit(solution)/shard_map/dot_general | solution.py:21
  1210.2 0.0 all-gather.9.cloned.1.call-update
  1210.2 0.6 reduce-scatter.13.cloned.1.call-start
  1210.8 35.7 %convolution_bitcast_fusion = f32[1280,2560]{0,1:T(8,128)} fusion(bf16[4096,2560]{1,0:T(8,128)(2,1)} %get-tuple-element.14, bf16[4096,1280]{1,0:T(8,128)(2,1)} %all-gather.5.cloned.1.call-done), kind=kOutput, calls=%fused_computation.10 | convolution fusion | flops 26843545600 | bytes 44564480 | tf_op jit(solution)/shard_map/dot_general | solution.py:31
  1246.5 14.0 copy.10
  1260.5 0.0 reduce-scatter.13.cloned.1.call-update
  1260.5 0.2 reduce-scatter.11.cloned.1.call-start
  1260.7 432.7 %all-gather.9.cloned.1.call-done = bf16[4096,5120]{1,0:T(8,128)(2,1)} async-done(((bf16[4096,2560]{1,0:T(8,128)(2,1)}), bf16[4096,5120]{1,0:T(8,128)(2,1)}) %all-gather.9.cloned.1.call-update) | async-done | bytes 41943056 | tf_op jit(solution)/shard_map/all_gather | solution.py:24
  1693.4 41.1 %fusion.9 = f32[5120,640]{1,0:T(8,128)} fusion(bf16[4096,5120]{1,0:T(8,128)(2,1)} %all-gather.9.cloned.1.call-done, bf16[4096,640]{1,0:T(8,128)(2,1)} %param.7), kind=kOutput, calls=%fused_computation.14 | convolution fusion | flops 26843545600 | bytes 60293120 | tf_op jit(solution)/shard_map/dot_general | solution.py:34
  1734.5 0.0 reduce-scatter.11.cloned.1.call-update
  1734.5 0.0 reduce-scatter.9.cloned.1.call-start
  1734.6 34.6 %fusion.8 = f32[4096,1280]{1,0:T(8,128)} fusion(bf16[4096,2560]{1,0:T(8,128)(2,1)} %get-tuple-element.14, bf16[1280,2560]{1,0:T(8,128)(2,1)} %all-gather.7.cloned.1.call-done), kind=kOutput, calls=%fused_computation.13 | convolution fusion | flops 26843545600 | bytes 48496640 | tf_op jit(solution)/shard_map/dot_general | solution.py:29
  1769.2 0.0 reduce-scatter.9.cloned.1.call-update
  1769.2 0.3 all-reduce.3.cloned.1.call-start
  1769.5 21.9 reduce-scatter.13.cloned.1.call-done
  1791.4 5.0 copy.11
  1796.5 93.1 %reduce-scatter.11.cloned.1.call-done = f32[1280,640]{1,0:T(8,128)} async-done(((f32[5120,640]{1,0:T(8,128)}), f32[1280,640]{1,0:T(8,128)}) %reduce-scatter.11.cloned.1.call-update) | async-done | bytes 3276816 | tf_op jit(solution)/shard_map/reduce_scatter | solution.py:35
  1889.6 0.0 all-reduce.3.cloned.1.call-update
  1889.6 234.6 %reduce-scatter.9.cloned.1.call-done = f32[4096,640]{1,0:T(8,128)} async-done(((f32[4096,1280]{1,0:T(8,128)}), f32[4096,640]{1,0:T(8,128)}) %reduce-scatter.9.cloned.1.call-update) | async-done | bytes 10485776 | tf_op jit(solution)/shard_map/reduce_scatter | solution.py:30
  2124.3 6.9 convert_element_type.15
  2131.1 39.7 %convolution_convert_fusion = bf16[4096,640]{1,0:T(8,128)(2,1)} fusion(bf16[4096,5120]{1,0:T(8,128)(2,1)} %all-gather.9.cloned.1.call-done, bf16[5120,640]{1,0:T(8,128)(2,1)} %all-gather.11.cloned.1.call-done), kind=kOutput, calls=%fused_computation.11 | convolution fusion | flops 26846167040 | bytes 53739520 | tf_op jit(solution)/shard_map/dot_general | solution.py:25
  2170.9 125.0 %all-reduce.3.cloned.1.call-done = (f32[320,2560]{0,1:T(8,128)}, f32[1280,640]{1,0:T(8,128)}) async-done(((f32[320,2560]{0,1:T(8,128)}, f32[1280,640]{1,0:T(8,128)}), (f32[320,2560]{0,1:T(8,128)}, f32[1280,640]{1,0:T(8,128)})) %all-reduce.3.cloned.1.call-update) | async-done | bytes 6553616 | tf_op jit(solution)/shard_map/psum | solution.py:33
  2295.8 5.2 copy.9
  2301.1 3.8 copy.14
Async XLA Ops:
  7.2 51.2 %all-gather.11.cloned.1.call-start = ((), (), s32[]{:S(2)}) async-start(), calls=%async_computation.7 | async-start | bytes 8192000 | tf_op jit(solution)/shard_map/all_gather | solution.py:20
  7.9 98.1 %all-gather.7.cloned.1.call-start = ((), (), s32[]{:S(2)}) async-start(), calls=%async_computation.5 | async-start | bytes 8192000 | tf_op jit(solution)/shard_map/all_gather | solution.py:19
  8.6 227.4 %all-gather.5.cloned.1.call-start = ((), (), s32[]{:S(2)}) async-start(), calls=%async_computation.4 | async-start | bytes 15728640 | tf_op jit(solution)/shard_map/all_gather | solution.py:18
  9.4 1135.3 %reduce-scatter.7.cloned.1.call-start = ((), (), s32[]{:S(2)}) async-start(), calls=%async_computation.8 | async-start | bytes 125829120 | tf_op jit(solution)/shard_map/reduce_scatter | solution.py:27
  102.2 1591.2 %all-gather.9.cloned.1.call-start = ((), (), s32[]{:S(2)}) async-start(), calls=%async_computation.6 | async-start | bytes 62914560 | tf_op jit(solution)/shard_map/all_gather | solution.py:24
  1210.2 581.2 %reduce-scatter.13.cloned.1.call-start = ((), (), s32[]{:S(2)}) async-start(), calls=%async_computation.11 | async-start | bytes 16384000
  1260.5 629.1 %reduce-scatter.11.cloned.1.call-start = ((), (), s32[]{:S(2)}) async-start(), calls=%async_computation.10 | async-start | bytes 16384000 | tf_op jit(solution)/shard_map/reduce_scatter | solution.py:35
  1734.5 389.7 %reduce-scatter.9.cloned.1.call-start = ((), (), s32[]{:S(2)}) async-start(), calls=%async_computation.9 | async-start | bytes 31457280 | tf_op jit(solution)/shard_map/reduce_scatter | solution.py:30
  1769.2 526.6 %all-reduce.3.cloned.1.call-start = ((), (), s32[]{:S(2)}) async-start(), calls=%async_computation.12 | async-start | bytes 14417920 | tf_op jit(solution)/shard_map/psum | solution.py:33
Sparse Core Ops, SparseCore 0:
  9.5 48.8 all-gather.10
  59.9 46.0 all-gather.6
  107.6 128.4 all-gather.4
  238.2 906.4 reduce-scatter.6
  1210.3 483.0 all-gather.8
  1695.8 95.5 reduce-scatter.12
  1794.0 95.5 reduce-scatter.10
  1891.9 232.3 reduce-scatter.8
  2126.8 169.0 all-reduce.2
where the time goes:
time: 2320 us; the launch traced here: 2310 us
  waiting for transfers between devices  2000 us (86%)
  matrix products  261 us (11%)
  local copies, waits for them, and re-layouts  28.1 us (1%)
    reduce_scatter x1, waiting for transfers between devices, local_block(): lax.psum_scatter(d_hidden_part, 'col', scatter_dimension=1, tiled=True)  909 us
    all_gather x1, waiting for transfers between devices, local_block(): hidden_full = lax.all_gather(hidden, 'col', axis=1, tiled=True)  433 us
    reduce_scatter x1, waiting for transfers between devices, local_block(): lax.psum_scatter(dx_part, 'col', scatter_dimension=1, tiled=True)  235 us
    all_gather x1, waiting for transfers between devices, local_block(): tok_full = lax.all_gather(tok_blk, 'col', axis=1, tiled=True)  130 us
    psum x1, waiting for transfers between devices, local_block(): dw_up = lax.psum(dw_up_layer, 'depth')  125 us
    reduce_scatter x1, waiting for transfers between devices, local_block(): lax.psum_scatter(dw_down_part, 'row', scatter_dimension=0, tiled=True)  93.1 us
    dot_general x1, matrix products, local_block(): pre_act = jnp.dot(tok_full, up_cols, preferred_element_type=jnp.float32)  65.5 us
    all_gather x1, waiting for transfers between devices, local_block(): down_cols = lax.all_gather(down_blk, 'row', axis=0, tiled=True)  49 us
  transfers between devices with their start and end apart: 9, of which 9 were waited for; matrix products, arithmetic and copies ran while one was open for 10% of the time, Pallas kernels for 0%

commit v1 on v0

v1 whole, which is shorter than its diff:
```python
import jax
import jax.numpy as jnp
from jax import lax
from jax.experimental import pallas as pl
from jax.experimental.pallas import tpu as pltpu
from jax.sharding import PartitionSpec as P


BF16, F32 = jnp.bfloat16, jnp.float32
VMEM_LIMIT = 60 * 1024 * 1024
SQRT_2_OVER_PI = 0.7978845608028654
CUBIC = 0.044715
NCHUNK = 4
NPIECE = 4
LAST_LAST = (((1,), (1,)), ((), ()))


def dot(a, b):
    return jnp.dot(a, b, preferred_element_type=F32)


def dot_t(a, b):
    return lax.dot_general(a, b, LAST_LAST, preferred_element_type=F32)


def cost(flops, nbytes, trans=0):
    return pl.CostEstimate(flops=flops, bytes_accessed=nbytes, transcendentals=trans)


def params():
    return pltpu.CompilerParams(vmem_limit_bytes=VMEM_LIMIT)


def up_body(s_ref, xo_ref, xt_ref, wo_ref, wt_ref, *rest):
    a_ref, d_ref = rest[-2:]
    rows = xo_ref.shape[0]
    sub = 256
    for i in range(rows // sub):
        sl = pl.ds(i * sub, sub)
        u = dot(xo_ref[sl, :], wo_ref[...]) + dot(xt_ref[sl, :], wt_ref[...])
        u2 = u * u
        t = jnp.tanh(u * (SQRT_2_OVER_PI + (SQRT_2_OVER_PI * CUBIC) * u2))
        h = 0.5 + 0.5 * t
        a_ref[sl, :] = (u * h).astype(BF16)
        slope = SQRT_2_OVER_PI + (3.0 * SQRT_2_OVER_PI * CUBIC) * u2
        d_ref[sl, :] = h + ((1.0 - t * t) * (0.5 * u)) * slope


def up_kernel(s, x_own, x_oth, w1, chunk, bufs, bn=512):
    tokens, hh = x_own.shape
    rows = x_oth.shape[0]
    f = w1.shape[1]
    in_specs = [
        pl.BlockSpec((rows, hh), lambda j, s: (chunk, 0)),
        pl.BlockSpec((rows, hh), lambda j, s: (0, 0)),
        pl.BlockSpec((hh, bn), lambda j, s: (s[0], j)),
        pl.BlockSpec((hh, bn), lambda j, s: (1 - s[0], j)),
    ]
    out_spec = pl.BlockSpec((rows, bn), lambda j, s: (chunk, j))
    args = [s, x_own, x_oth, w1, w1]
    aliases = {}
    if bufs is not None:
        in_specs += [pl.BlockSpec(memory_space=pl.ANY)] * 2
        args += list(bufs)
        aliases = {5: 0, 6: 1}
    return pl.pallas_call(
        up_body,
        grid_spec=pltpu.PrefetchScalarGridSpec(
            num_scalar_prefetch=1, grid=(f // bn,), in_specs=in_specs, out_specs=[out_spec, out_spec]),
        out_shape=[jax.ShapeDtypeStruct((tokens, f), BF16), jax.ShapeDtypeStruct((tokens, f), F32)],
        input_output_aliases=aliases,
        compiler_params=params(),
        cost_estimate=cost(2 * rows * 2 * hh * f, rows * f * 6 + 2 * hh * f * 2, rows * f),
        name="up",
    )(*args)


def du_body(go_ref, gt_ref, wo_ref, wt_ref, d_ref, *rest):
    u_ref = rest[-1]
    rows = go_ref.shape[0]
    sub = 256
    for i in range(rows // sub):
        sl = pl.ds(i * sub, sub)
        da = dot_t(go_ref[sl, :], wo_ref[...]) + dot_t(gt_ref[sl, :], wt_ref[...])
        u_ref[sl, :] = (da * d_ref[sl, :]).astype(BF16)


def du_kernel(g_own, g_oth, w2_own, w2_oth, d, chunk, buf, bn=512):
    tokens, hh = g_own.shape
    rows = g_oth.shape[0]
    f = w2_own.shape[0]
    in_specs = [
        pl.BlockSpec((rows, hh), lambda j: (chunk, 0)),
        pl.BlockSpec((rows, hh), lambda j: (0, 0)),
        pl.BlockSpec((bn, hh), lambda j: (j, 0)),
        pl.BlockSpec((bn, hh), lambda j: (j, 0)),
        pl.BlockSpec((rows, bn), lambda j: (chunk, j)),
    ]
    args = [g_own, g_oth, w2_own, w2_oth, d]
    aliases = {}
    if buf is not None:
        in_specs.append(pl.BlockSpec(memory_space=pl.ANY))
        args.append(buf)
        aliases = {5: 0}
    return pl.pallas_call(
        du_body,
        grid=(f // bn,),
        in_specs=in_specs,
        out_specs=pl.BlockSpec((rows, bn), lambda j: (chunk, j)),
        out_shape=jax.ShapeDtypeStruct((tokens, f), BF16),
        input_output_aliases=aliases,
        compiler_params=params(),
        cost_estimate=cost(2 * rows * 2 * hh * f, rows * f * 6 + 2 * hh * f * 2),
        name="du",
    )(*args)


def y_body(a_ref, w_ref, o_ref):
    o_ref[...] = dot(a_ref[...], w_ref[...]).astype(BF16)


def y_kernel(a, w2_own, bm=512):
    tokens, f = a.shape
    n = w2_own.shape[1]
    return pl.pallas_call(
        y_body,
        grid=(tokens // bm,),
        in_specs=[pl.BlockSpec((bm, f), lambda i: (i, 0)), pl.BlockSpec((f, n), lambda i: (0, 0))],
        out_specs=pl.BlockSpec((bm, n), lambda i: (i, 0)),
        out_shape=jax.ShapeDtypeStruct((tokens, n), BF16),
        compiler_params=params(),
        cost_estimate=cost(2 * tokens * f * n, tokens * f * 2 + f * n * 2),
        name="y",
    )(a, w2_own)


def dx_body(s_ref, u_ref, w_ref, o_ref):
    o_ref[...] = dot_t(u_ref[...], w_ref[...]).astype(BF16)


def dx_kernel(s, du, w1, hh, bm=512):
    tokens, f = du.shape
    return pl.pallas_call(
        dx_body,
        grid_spec=pltpu.PrefetchScalarGridSpec(
            num_scalar_prefetch=1,
            grid=(tokens // bm,),
            in_specs=[
                pl.BlockSpec((bm, f), lambda i, s: (i, 0)),
                pl.BlockSpec((hh, f), lambda i, s: (s[0], 0)),
            ],
            out_specs=pl.BlockSpec((bm, hh), lambda i, s: (i, 0))),
        out_shape=jax.ShapeDtypeStruct((tokens, hh), BF16),
        compiler_params=params(),
        cost_estimate=cost(2 * tokens * f * hh, tokens * f * 2 + f * hh * 2),
        name="dx",
    )(s, du, w1)


def dw2_body(s_ref, g_ref, a_ref, o_ref):
    o_ref[...] = dot(g_ref[...], a_ref[...])


def dw2_kernel(idx, g_t, a, width, bn=256):
    n, tokens = g_t.shape
    steps = width // bn
    return pl.pallas_call(
        dw2_body,
        grid_spec=pltpu.PrefetchScalarGridSpec(
            num_scalar_prefetch=1,
            grid=(steps,),
            in_specs=[
                pl.BlockSpec((n, tokens), lambda j, s: (0, 0)),
                pl.BlockSpec((tokens, bn), lambda j, s: (0, s[0] * steps + j)),
            ],
            out_specs=pl.BlockSpec((n, bn), lambda j, s: (0, j))),
        out_shape=jax.ShapeDtypeStruct((n, width), F32),
        compiler_params=params(),
        cost_estimate=cost(2 * tokens * n * width, tokens * (n + width) * 2 + n * width * 4),
        name="dw2",
    )(idx, g_t, a)


def dw1_body(s_ref, x_ref, u_ref, mine_ref, theirs_ref):
    r = dot(x_ref[...], u_ref[...])
    half = r.shape[0] // 2

    @pl.when(s_ref[2] == 0)
    def _():
        mine_ref[...] = r[:half]
        theirs_ref[...] = r[half:]

    @pl.when(s_ref[2] != 0)
    def _():
        mine_ref[...] = r[half:]
        theirs_ref[...] = r[:half]


def dw1_kernel(s, x_t, du, width, part, nparts, bn=256):
    hrows, tokens = x_t.shape
    half = hrows // 2
    steps = width // nparts // bn
    out_spec = pl.BlockSpec((half // 2, bn), lambda j, s: (0, j))
    shape = jax.ShapeDtypeStruct((half // 2, width // nparts), F32)
    return pl.pallas_call(
        dw1_body,
        grid_spec=pltpu.PrefetchScalarGridSpec(
            num_scalar_prefetch=1,
            grid=(steps,),
            in_specs=[
                pl.BlockSpec((half, tokens), lambda j, s: (s[0], 0)),
                pl.BlockSpec((tokens, bn), lambda j, s: (0, (s[1] * nparts + part) * steps + j)),
            ],
            out_specs=[out_spec, out_spec]),
        out_shape=[shape, shape],
        compiler_params=params(),
        cost_estimate=cost(2 * tokens * half * width // nparts, tokens * (half + width // nparts) * 2 + half * width * 4 // nparts),
        name="dw1",
    )(s, x_t, du)


def solution(mesh):
    nx = mesh.shape["row"] // 2
    act_spec = P(("depth", "row"), "col")
    weight_spec = P("row", "col")
    pair = [(0, 1), (1, 0)]
    core_pair = [(r, r ^ 1) for r in range(2 * nx)]
    x_pair = [(r, r ^ 2) for r in range(2 * nx)]

    def over_core(v):
        return lax.ppermute(v, "row", core_pair)

    def over_x(v):
        return lax.ppermute(v, "row", x_pair)

    def over_col(v):
        return lax.ppermute(v, "col", pair)

    def over_depth(v):
        return lax.ppermute(v, "depth", pair)

    def body(tok, up, down, grad):
        col = lax.axis_index("col")
        row = lax.axis_index("row")
        depth = lax.axis_index("depth")
        x, core = row // 2, row % 2
        tokens, hh = tok.shape
        rows = tokens // NCHUNK
        fh = up.shape[1]

        def half_block(blk):
            n = blk.shape[0] // 2
            return lax.dynamic_slice_in_dim(blk, depth * n, n, 0)

        def other_block(blk):
            first = over_col(half_block(blk))
            second = over_depth(first)
            lo = jnp.where(depth == 0, first, second)
            hi = jnp.where(depth == 0, second, first)
            return jnp.concatenate([lo, hi], axis=0)

        def row_blocks(blk):
            b_c = over_core(blk)
            b_x = over_x(blk)
            b_xc = over_core(b_x)
            return ((row, blk), (row ^ 1, b_c), (row ^ 2, b_x), (row ^ 3, b_xc))

        up_oth = other_block(up)
        tok_oth = []
        grad_oth = []
        for i in range(NCHUNK):
            tok_oth.append(over_col(tok[i * rows:(i + 1) * rows]))
        down_oth = other_block(down)
        for i in range(NCHUNK):
            grad_oth.append(over_col(grad[i * rows:(i + 1) * rows]))

        w1 = jnp.zeros((4 * up.shape[0], 2 * fh), BF16)
        for r, b in row_blocks(up):
            w1 = lax.dynamic_update_slice(w1, b, (r * up.shape[0], col * fh))
        for r, b in row_blocks(up_oth):
            w1 = lax.dynamic_update_slice(w1, b, (r * up.shape[0], (1 - col) * fh))
        w2_own = jnp.zeros((4 * down.shape[0], hh), BF16)
        for r, b in row_blocks(down):
            w2_own = lax.dynamic_update_slice(w2_own, b, (r * down.shape[0], 0))
        w2_oth = jnp.zeros((4 * down.shape[0], hh), BF16)
        for r, b in row_blocks(down_oth):
            w2_oth = lax.dynamic_update_slice(w2_oth, b, (r * down.shape[0], 0))

        grad_t = grad.T
        x_t = jnp.zeros((2 * hh, tokens), BF16)
        x_t = lax.dynamic_update_slice(x_t, tok.T, (col * hh, 0))
        for i in range(NCHUNK):
            x_t = lax.dynamic_update_slice(x_t, tok_oth[i].T, ((1 - col) * hh, i * rows))

        scol = jnp.stack([col])
        bufs = None
        for i in range(NCHUNK):
            bufs = up_kernel(scol, tok, tok_oth[i], w1, i, bufs)
        a, d = bufs

        fb = down.shape[0]
        parts = {}
        for q in (3, 2, 1, 0):
            parts[q] = dw2_kernel(jnp.stack([row ^ q]), grad_t, a, fb)
        got3 = over_core(parts[3])
        got1 = over_core(parts[1])
        n = hh // NPIECE
        pieces = []
        for p in range(NPIECE):
            sl = slice(p * n, (p + 1) * n)
            away = parts[2][sl] + got3[sl]
            came = over_x(away)
            layer = (parts[0][sl] + got1[sl]) + came
            pieces.append((layer + over_depth(layer)).T)
        dw_down = jnp.concatenate(pieces, axis=1)

        du = None
        for i in range(NCHUNK):
            du = du_kernel(grad, grad_oth[i], w2_own, w2_oth, d, i, du)

        nparts = 2
        s_away = jnp.stack([1 - x, col, core])
        s_here = jnp.stack([x, col, core])
        away = [dw1_kernel(s_away, x_t, du, fh, p, nparts) for p in range(nparts)]
        here = [dw1_kernel(s_here, x_t, du, fh, p, nparts) for p in range(nparts)]
        cols = []
        per = NPIECE // nparts
        for p in range(nparts):
            got_away = over_core(away[p][1])
            got_here = over_core(here[p][1])
            w = fh // NPIECE
            for q in range(per):
                sl = slice(q * w, (q + 1) * w)
                out = away[p][0][:, sl] + got_away[:, sl]
                came = over_x(out)
                layer = (here[p][0][:, sl] + got_here[:, sl]) + came
                cols.append(layer + over_depth(layer))
        dw_up = jnp.concatenate(cols, axis=1)

        out_blk = y_kernel(a, w2_own)
        dx_blk = dx_kernel(scol, du, w1, hh)
        return out_blk, dx_blk, dw_up, dw_down

    return jax.shard_map(body, mesh=mesh, in_specs=(act_spec, weight_spec, weight_spec, act_spec),
                         out_specs=(act_spec, act_spec, weight_spec, weight_spec), check_vma=False)
```

time: 2320 us -> 898 us (0.39)
  waiting for transfers between devices: 2000 us -> 226 us
  Pallas kernels: 0 us -> 399 us
  matrix products: 261 us -> 0 us
  local copies, waits for them, and re-layouts: 28.1 us -> 182 us
  starting transfers between devices: 1.56 us -> 40.6 us
  other arithmetic: 6.88 us -> 35.9 us
    reduce_scatter x3 -> x0, waiting for transfers between devices: 1240 us -> none  [the longest x1 909 us: local_block(): lax.psum_scatter(d_hidden_part, 'col', scatter_dimension=1, tiled=True)]
    all_gather x4 -> x0, waiting for transfers between devices: 615 us -> none  [the longest x1 433 us: local_block(): hidden_full = lax.all_gather(hidden, 'col', axis=1, tiled=True)]
    pallas_call x0 -> x18, Pallas kernels: none -> 399 us  [the longest x4 119 us: up_kernel(): pl.pallas_call(up_body, grid_spec=pltpu.PrefetchScalarGridSpec(num_scalar...]
    dot_general x6 -> x0, matrix products: 261 us -> none  [the longest x1 65.5 us: local_block(): pre_act = jnp.dot(tok_full, up_cols, preferred_element_type=jnp.float32)]
    ppermute x0 -> x46, waiting for transfers between devices: none -> 226 us  [the longest x12 135 us: over_x(): return lax.ppermute(v, 'row', x_pair)]
    psum x1 -> x0, waiting for transfers between devices: 125 us -> none  [local_block(): dw_up = lax.psum(dw_up_layer, 'depth')]
    dynamic_update_slice x0 -> x19, local copies, waits for them, and re-layouts: none -> 124 us  [the longest x4 58.5 us: body(): w1 = lax.dynamic_update_slice(w1, b, (r * up.shape[0], col * fh))]
    ppermute x0 -> x46, starting transfers between devices: none -> 40.6 us  [the longest x12 15.6 us: over_x(): return lax.ppermute(v, 'row', x_pair)]
  transfers between devices with their start and end apart: 9 -> 46, of which waited for: 9 -> 15; matrix products, arithmetic and copies ran while one was open for 10% -> 24% of each run, Pallas kernels for 0% -> 45%
where the time goes in v1:
time: 898 us; the launch traced here: 884 us
  Pallas kernels  399 us (44%)
  waiting for transfers between devices  226 us (25%)
  local copies, waits for them, and re-layouts  182 us (20%)
  starting transfers between devices  40.6 us (5%)
  other arithmetic  35.9 us (4%)
    ppermute x12, waiting for transfers between devices, over_x(): return lax.ppermute(v, 'row', x_pair)  135 us
    pallas_call x4, Pallas kernels, up_kernel(): pl.pallas_call(up_body, grid_spec=pltpu.PrefetchScalarGridSpec(num_scalar...  119 us
    pallas_call x4, Pallas kernels, du_kernel(): pl.pallas_call(du_body, grid=(f // bn,), in_specs=in_specs, out_specs=pl....  99.9 us
    dynamic_update_slice x4, local copies, waits for them, and re-layouts, body(): w1 = lax.dynamic_update_slice(w1, b, (r * up.shape[0], col * fh))  58.5 us
    pallas_call x4, Pallas kernels, dw1_kernel(): pl.pallas_call(dw1_body, grid_spec=pltpu.PrefetchScalarGridSpec(num_scala...  52.3 us
    pallas_call x4, Pallas kernels, dw2_kernel(): pl.pallas_call(dw2_body, grid_spec=pltpu.PrefetchScalarGridSpec(num_scala...  49.3 us
    ppermute x10, waiting for transfers between devices, over_depth(): return lax.ppermute(v, 'depth', pair)  46.8 us
    ppermute x10, waiting for transfers between devices, over_col(): return lax.ppermute(v, 'col', pair)  43.9 us
  transfers between devices with their start and end apart: 46, of which 15 were waited for; matrix products, arithmetic and copies ran while one was open for 24% of the time, Pallas kernels for 45%

profile of v1, /device:TPU:0, one launch (start us, length us, event | category | flops | bytes accessed | tf_op | source)
XLA Modules:
  0.0 884.3 jit_solution(12055212803391518691)
XLA Ops:
  0.6 3.2 collective-permute-start.2
  7.5 7.8 copy.17
  15.4 5.0 fusion.10
  24.5 2.8 collective-permute-done.4
  28.9 11.1 %collective-permute-done.2 = bf16[320,2560]{1,0:T(8,128)(2,1)} collective-permute-done((bf16[320,2560]{1,0:T(8,128)(2,1)}, bf16[320,2560]{1,0:T(8,128)(2,1)}, u32[]{:S(2)}, u32[]{:S(2)}) %collective-permute-start.2) | collective-permute-done | bytes 1638432 | tf_op jit(solution)/shard_map/ppermute | solution.py:234
  40.0 5.1 broadcast_in_dim.7
  45.1 2.6 bitcast_dynamic-update-slice_fusion
  47.7 23.9 %collective-permute-done.16 = bf16[640,640]{1,0:T(8,128)(2,1)} collective-permute-done((bf16[640,640]{1,0:T(8,128)(2,1)}, bf16[640,640]{1,0:T(8,128)(2,1)}, u32[]{:S(2)}, u32[]{:S(2)}) %collective-permute-start.16) | collective-permute-done | bytes 819232 | tf_op jit(solution)/shard_map/ppermute | solution.py:237
  73.2 3.3 broadcast.5.clone
  76.5 2.8 constant_dynamic-update-slice_fusion.7
  79.3 7.8 copy.26
  87.2 6.4 broadcast_in_dim.6
  93.6 14.9 %dynamic_update_slice.63 = bf16[1280,5120]{1,0:T(8,128)(2,1)} dynamic-update-slice(bf16[1280,5120]{1,0:T(8,128)(2,1)} %broadcast_in_dim.6, bf16[320,2560]{1,0:T(8,128)(2,1)} %param.5, s32[]{:T(128)S(6)} %select_n.94, s32[]{:T(128)S(6)} %select_n.95) | dynamic-update-slice | bytes 3276804 | tf_op jit(solution)/shard_map/dynamic_update_slice | solution.py:279
  114.3 3.2 broadcast.5.clone.1
  119.5 14.7 %dynamic_update_slice.64 = bf16[1280,5120]{1,0:T(8,128)(2,1)} dynamic-update-slice(bf16[1280,5120]{1,0:T(8,128)(2,1)} %dynamic_update_slice.63, bf16[320,2560]{1,0:T(8,128)(2,1)} %collective-permute-done.1, s32[]{:T(128)S(6)} %select_n.96, s32[]{:T(128)S(6)} %select_n.95) | dynamic-update-slice | bytes 3276804 | tf_op jit(solution)/shard_map/dynamic_update_slice | solution.py:279
  134.2 15.1 %dynamic_update_slice.65 = bf16[1280,5120]{1,0:T(8,128)(2,1)} dynamic-update-slice(bf16[1280,5120]{1,0:T(8,128)(2,1)} %dynamic_update_slice.64, bf16[320,2560]{1,0:T(8,128)(2,1)} %collective-permute-done.2, s32[]{:T(128)S(6)} %select_n.97, s32[]{:T(128)S(6)} %select_n.95) | dynamic-update-slice | bytes 3276804 | tf_op jit(solution)/shard_map/dynamic_update_slice | solution.py:279
  149.3 13.9 %dynamic_update_slice.66 = bf16[1280,5120]{1,0:T(8,128)(2,1)} dynamic-update-slice(bf16[1280,5120]{1,0:T(8,128)(2,1)} %dynamic_update_slice.65, bf16[320,2560]{1,0:T(8,128)(2,1)} %collective-permute-done.3, s32[]{:T(128)S(6)} %select_n.98, s32[]{:T(128)S(6)} %select_n.95) | dynamic-update-slice | bytes 3276804 | tf_op jit(solution)/shard_map/dynamic_update_slice | solution.py:279
  169.5 2.5 fusion.9
  173.4 2.5 copy.22.xt_ref
  178.3 15.5 %collective-permute-done = bf16[1024,640]{0,1:T(8,128)(2,1)} collective-permute-done((bf16[1024,640]{0,1:T(8,128)(2,1)}, bf16[1024,640]{0,1:T(8,128)(2,1)}, u32[]{:S(2)}, u32[]{:S(2)}) %collective-permute-start) | collective-permute-done | bytes 1310752 | tf_op jit(solution)/shard_map/ppermute | solution.py:237
  193.8 2.4 copy.24.xt_ref
  197.4 2.5 bitcast_dynamic-update-slice_fusion.3
  200.5 2.6 bitcast_dynamic-update-slice_fusion.2
  203.6 2.5 bitcast_dynamic-update-slice_fusion.1.x_ref
  206.1 30.8 %collective-permute-done.7 = bf16[320,2560]{1,0:T(8,128)(2,1)} collective-permute-done((bf16[320,2560]{1,0:T(8,128)(2,1)}, bf16[320,2560]{1,0:T(8,128)(2,1)}, u32[]{:S(2)}, u32[]{:S(2)}) %collective-permute-start.7) | collective-permute-done | bytes 1638432 | tf_op jit(solution)/shard_map/ppermute | solution.py:234
  236.9 2.8 constant_dynamic-update-slice_fusion.6
  239.6 2.7 constant_dynamic-update-slice_fusion.5
  243.7 2.8 constant_dynamic-update-slice_fusion.1
  249.8 13.0 %dynamic_update_slice.68 = bf16[1280,5120]{1,0:T(8,128)(2,1)} dynamic-update-slice(bf16[1280,5120]{1,0:T(8,128)(2,1)} %get-tuple-element.69, bf16[320,2560]{1,0:T(8,128)(2,1)S(1)} %collective-permute-done.6, s32[]{:T(128)S(6)} %select_n.96, s32[]{:T(128)S(6)} %select_n.103) | dynamic-update-slice | bytes 3276804 | tf_op jit(solution)/shard_map/dynamic_update_slice | solution.py:281
  262.8 13.9 %dynamic_update_slice.69 = bf16[1280,5120]{1,0:T(8,128)(2,1)} dynamic-update-slice(bf16[1280,5120]{1,0:T(8,128)(2,1)} %dynamic_update_slice.68, bf16[320,2560]{1,0:T(8,128)(2,1)} %collective-permute-done.7, s32[]{:T(128)S(6)} %select_n.97, s32[]{:T(128)S(6)} %select_n.103) | dynamic-update-slice | bytes 3276804 | tf_op jit(solution)/shard_map/dynamic_update_slice | solution.py:281
  276.7 3.7 collective-permute-start.15
  281.8 12.2 %dynamic_update_slice.70.wo_ref.wt_ref.w_ref = bf16[1280,5120]{1,0:T(8,128)(2,1)} dynamic-update-slice(bf16[1280,5120]{1,0:T(8,128)(2,1)} %dynamic_update_slice.69, bf16[320,2560]{1,0:T(8,128)(2,1)S(1)} %collective-permute-done.8, s32[]{:T(128)S(6)} %select_n.98, s32[]{:T(128)S(6)} %select_n.103) | dynamic-update-slice | bytes 3276804 | tf_op jit(solution)/shard_map/dynamic_update_slice | solution.py:281
  294.0 29.9 %up.4 = (bf16[4096,5120]{1,0:T(8,128)(2,1)}, f32[4096,5120]{1,0:T(8,128)}) custom-call(s32[1]{0:T(128)} %bitcast.s_ref, bf16[4096,640]{1,0:T(8,128)(2,1)} %xo_ref.7, bf16[1024,640]{1,0:T(8,128)(2,1)} %copy.21.xt_ref, bf16[1280,5120]{1,0:T(8,128)(2,1)} %dynamic_update_slice.70.wo_ref.wt_ref.w_ref, bf16[1280,5120]{1,0:T(8,128)(2,1)} %dynamic_update_slice.70.wo_ref.wt_ref.w_ref), custom_call_target="tpu_custom_call" | custom-call | flops 13421772800 | bytes 44564480 | tf_op jit(solution)/shard_map/up/pallas_call | solution.py:66
  323.9 29.6 %up.5 = (bf16[4096,5120]{1,0:T(8,128)(2,1)}, f32[4096,5120]{1,0:T(8,128)}) custom-call(s32[1]{0:T(128)} %bitcast.s_ref, bf16[4096,640]{1,0:T(8,128)(2,1)} %xo_ref.7, bf16[1024,640]{1,0:T(8,128)(2,1)} %copy.22.xt_ref, bf16[1280,5120]{1,0:T(8,128)(2,1)} %dynamic_update_slice.70.wo_ref.wt_ref.w_ref, ...), custom_call_target="tpu_custom_call", output_to_operand_aliasing={{0}: (5, {}), {1}: (6, {})} | custom-call | flops 13421772800 | bytes 44564480 | tf_op jit(solution)/shard_map/up/pallas_call | solution.py:66
  353.5 29.5 %up.6 = (bf16[4096,5120]{1,0:T(8,128)(2,1)}, f32[4096,5120]{1,0:T(8,128)}) custom-call(s32[1]{0:T(128)} %bitcast.s_ref, bf16[4096,640]{1,0:T(8,128)(2,1)} %xo_ref.7, bf16[1024,640]{1,0:T(8,128)(2,1)} %copy.23.xt_ref, bf16[1280,5120]{1,0:T(8,128)(2,1)} %dynamic_update_slice.70.wo_ref.wt_ref.w_ref, ...), custom_call_target="tpu_custom_call", output_to_operand_aliasing={{0}: (5, {}), {1}: (6, {})} | custom-call | flops 13421772800 | bytes 44564480 | tf_op jit(solution)/shard_map/up/pallas_call | solution.py:66
  383.1 29.5 %up.7 = (bf16[4096,5120]{1,0:T(8,128)(2,1)}, f32[4096,5120]{1,0:T(8,128)}) custom-call(s32[1]{0:T(128)} %bitcast.s_ref, bf16[4096,640]{1,0:T(8,128)(2,1)} %xo_ref.7, bf16[1024,640]{1,0:T(8,128)(2,1)} %copy.24.xt_ref, bf16[1280,5120]{1,0:T(8,128)(2,1)} %dynamic_update_slice.70.wo_ref.wt_ref.w_ref, ...), custom_call_target="tpu_custom_call", output_to_operand_aliasing={{0}: (5, {}), {1}: (6, {})} | custom-call | flops 13421772800 | bytes 44564480 | tf_op jit(solution)/shard_map/up/pallas_call | solution.py:66
  412.6 12.3 %dw2.7 = f32[640,1280]{1,0:T(8,128)} custom-call(s32[1]{0:T(128)} %bitcast.13.s_ref, bf16[640,4096]{1,0:T(8,128)(2,1)} %bitcast.29, bf16[4096,5120]{1,0:T(8,128)(2,1)} %get-tuple-element.26.a_ref), custom_call_target="tpu_custom_call" | custom-call | flops 6710886400 | bytes 19005440 | tf_op jit(solution)/shard_map/dw2/pallas_call | solution.py:167
  424.9 25.1 %du.4.rest_0_ = bf16[4096,5120]{1,0:T(8,128)(2,1)} custom-call(bf16[4096,640]{1,0:T(8,128)(2,1)} %go_ref.7, bf16[1024,640]{1,0:T(8,128)(2,1)} %collective-permute-done.23.gt_ref, bf16[5120,640]{1,0:T(8,128)(2,1)} %constant_dynamic-update-slice_fusion.4.w_ref.wo_ref, bf16[5120,640]{1,0:T(8,128)(2,1)} %constant_dynamic-update-slice_fusion.wt_ref, ...), custom_call_target="tpu_custom_call" | custom-call | flops 13421772800 | bytes 44564480 | tf_op jit(solution)/shard_map/du/pallas_call | solution.py:105
  449.9 24.9 %du.5.rest_0_ = bf16[4096,5120]{1,0:T(8,128)(2,1)} custom-call(bf16[4096,640]{1,0:T(8,128)(2,1)} %go_ref.7, bf16[1024,640]{1,0:T(8,128)(2,1)} %collective-permute-done.22.gt_ref, bf16[5120,640]{1,0:T(8,128)(2,1)} %constant_dynamic-update-slice_fusion.4.w_ref.wo_ref, ...), custom_call_target="tpu_custom_call", output_to_operand_aliasing={{}: (5, {})} | custom-call | flops 13421772800 | bytes 44564480 | tf_op jit(solution)/shard_map/du/pallas_call | solution.py:105
  474.9 25.1 %du.6.rest_0_ = bf16[4096,5120]{1,0:T(8,128)(2,1)} custom-call(bf16[4096,640]{1,0:T(8,128)(2,1)} %go_ref.7, bf16[1024,640]{1,0:T(8,128)(2,1)} %collective-permute-done.21.gt_ref, bf16[5120,640]{1,0:T(8,128)(2,1)} %constant_dynamic-update-slice_fusion.4.w_ref.wo_ref, ...), custom_call_target="tpu_custom_call", output_to_operand_aliasing={{}: (5, {})} | custom-call | flops 13421772800 | bytes 44564480 | tf_op jit(solution)/shard_map/du/pallas_call | solution.py:105
  499.9 24.8 %du.7.u_ref = bf16[4096,5120]{1,0:T(8,128)(2,1)} custom-call(bf16[4096,640]{1,0:T(8,128)(2,1)} %go_ref.7, bf16[1024,640]{1,0:T(8,128)(2,1)} %collective-permute-done.15.gt_ref, bf16[5120,640]{1,0:T(8,128)(2,1)} %constant_dynamic-update-slice_fusion.4.w_ref.wo_ref, ...), custom_call_target="tpu_custom_call", output_to_operand_aliasing={{}: (5, {})} | custom-call | flops 13421772800 | bytes 44564480 | tf_op jit(solution)/shard_map/du/pallas_call | solution.py:105
  524.8 13.1 %dw1.4 = (f32[320,1280]{1,0:T(8,128)}, f32[320,1280]{1,0:T(8,128)}) custom-call(s32[3]{0:T(128)} %get-tuple-element.72.s_ref, bf16[1280,4096]{1,0:T(8,128)(2,1)} %bitcast_dynamic-update-slice_fusion.1.x_ref, bf16[4096,5120]{1,0:T(8,128)(2,1)} %du.7.u_ref), custom_call_target="tpu_custom_call" | custom-call | flops 6710886400 | bytes 19005440 | tf_op jit(solution)/shard_map/dw1/pallas_call | solution.py:205
  537.9 13.0 %dw1.5 = (f32[320,1280]{1,0:T(8,128)}, f32[320,1280]{1,0:T(8,128)}) custom-call(s32[3]{0:T(128)} %get-tuple-element.73.s_ref, bf16[1280,4096]{1,0:T(8,128)(2,1)} %bitcast_dynamic-update-slice_fusion.1.x_ref, bf16[4096,5120]{1,0:T(8,128)(2,1)} %du.7.u_ref), custom_call_target="tpu_custom_call" | custom-call | flops 6710886400 | bytes 19005440 | tf_op jit(solution)/shard_map/dw1/pallas_call | solution.py:205
  551.5 13.1 %dw1.6 = (f32[320,1280]{1,0:T(8,128)}, f32[320,1280]{1,0:T(8,128)}) custom-call(s32[3]{0:T(128)} %get-tuple-element.72.s_ref, bf16[1280,4096]{1,0:T(8,128)(2,1)} %bitcast_dynamic-update-slice_fusion.1.x_ref, bf16[4096,5120]{1,0:T(8,128)(2,1)} %du.7.u_ref), custom_call_target="tpu_custom_call" | custom-call | flops 6710886400 | bytes 19005440 | tf_op jit(solution)/shard_map/dw1/pallas_call | solution.py:205
  564.5 13.1 %dw1.7 = (f32[320,1280]{1,0:T(8,128)}, f32[320,1280]{1,0:T(8,128)}) custom-call(s32[3]{0:T(128)} %get-tuple-element.73.s_ref, bf16[1280,4096]{1,0:T(8,128)(2,1)} %bitcast_dynamic-update-slice_fusion.1.x_ref, bf16[4096,5120]{1,0:T(8,128)(2,1)} %du.7.u_ref), custom_call_target="tpu_custom_call" | custom-call | flops 6710886400 | bytes 19005440 | tf_op jit(solution)/shard_map/dw1/pallas_call | solution.py:205
  577.6 12.2 %dw2.5 = f32[640,1280]{1,0:T(8,128)} custom-call(s32[1]{0:T(128)} %bitcast.11.s_ref, bf16[640,4096]{1,0:T(8,128)(2,1)} %bitcast.30, bf16[4096,5120]{1,0:T(8,128)(2,1)} %get-tuple-element.26.a_ref), custom_call_target="tpu_custom_call" | custom-call | flops 6710886400 | bytes 19005440 | tf_op jit(solution)/shard_map/dw2/pallas_call | solution.py:167
  590.9 39.4 %dx.1 = bf16[4096,640]{1,0:T(8,128)(2,1)} custom-call(s32[1]{0:T(128)} %bitcast.s_ref, bf16[4096,5120]{1,0:T(8,128)(2,1)} %du.7.u_ref, bf16[1280,5120]{1,0:T(8,128)(2,1)} %dynamic_update_slice.70.wo_ref.wt_ref.w_ref), custom_call_target="tpu_custom_call" | custom-call | flops 26843545600 | bytes 48496640 | tf_op jit(solution)/shard_map/dx/pallas_call | solution.py:143
  630.3 3.3 slice_add_fusion.14
  635.1 2.9 slice_add_fusion.10
  640.6 12.5 %dw2.6 = f32[640,1280]{1,0:T(8,128)} custom-call(s32[1]{0:T(128)} %bitcast.12.s_ref, bf16[640,4096]{1,0:T(8,128)(2,1)} %bitcast.31, bf16[4096,5120]{1,0:T(8,128)(2,1)} %get-tuple-element.26.a_ref), custom_call_target="tpu_custom_call" | custom-call | flops 6710886400 | bytes 19005440 | tf_op jit(solution)/shard_map/dw2/pallas_call | solution.py:167
  653.1 4.7 slice_add_fusion.6
  659.2 13.4 %collective-permute-done.28 = f32[320,640]{1,0:T(8,128)} collective-permute-done((f32[320,640]{1,0:T(8,128)}, f32[320,640]{1,0:T(8,128)}, u32[]{:S(2)}, u32[]{:S(2)}) %collective-permute-start.28) | collective-permute-done | bytes 819232 | tf_op jit(solution)/shard_map/ppermute | solution.py:234
  674.1 16.1 %collective-permute-done.32 = f32[320,640]{1,0:T(8,128)} collective-permute-done((f32[320,640]{1,0:T(8,128)}, f32[320,640]{1,0:T(8,128)}, u32[]{:S(2)}, u32[]{:S(2)}) %collective-permute-start.32) | collective-permute-done | bytes 819232 | tf_op jit(solution)/shard_map/ppermute | solution.py:234
  691.6 16.1 %collective-permute-done.34 = f32[320,640]{1,0:T(8,128)} collective-permute-done((f32[320,640]{1,0:T(8,128)}, f32[320,640]{1,0:T(8,128)}, u32[]{:S(2)}, u32[]{:S(2)}) %collective-permute-start.34) | collective-permute-done | bytes 819232 | tf_op jit(solution)/shard_map/ppermute | solution.py:234
  709.2 12.4 %dw2.4 = f32[640,1280]{1,0:T(8,128)} custom-call(s32[1]{0:T(128)} %bitcast.9.s_ref, bf16[640,4096]{1,0:T(8,128)(2,1)} %bitcast.32, bf16[4096,5120]{1,0:T(8,128)(2,1)} %get-tuple-element.26.a_ref), custom_call_target="tpu_custom_call" | custom-call | flops 6710886400 | bytes 19005440 | tf_op jit(solution)/shard_map/dw2/pallas_call | solution.py:167
  728.4 14.5 %collective-permute-done.40 = f32[160,1280]{1,0:T(8,128)} collective-permute-done((f32[160,1280]{1,0:T(8,128)}, f32[160,1280]{1,0:T(8,128)}, u32[]{:S(2)}, u32[]{:S(2)}) %collective-permute-start.40) | collective-permute-done | bytes 819232 | tf_op jit(solution)/shard_map/ppermute | solution.py:234
  743.3 17.1 %collective-permute-done.42 = f32[160,1280]{1,0:T(8,128)} collective-permute-done((f32[160,1280]{1,0:T(8,128)}, f32[160,1280]{1,0:T(8,128)}, u32[]{:S(2)}, u32[]{:S(2)}) %collective-permute-start.42) | collective-permute-done | bytes 819232 | tf_op jit(solution)/shard_map/ppermute | solution.py:234
  760.9 16.2 %collective-permute-done.44 = f32[160,1280]{1,0:T(8,128)} collective-permute-done((f32[160,1280]{1,0:T(8,128)}, f32[160,1280]{1,0:T(8,128)}, u32[]{:S(2)}, u32[]{:S(2)}) %collective-permute-start.44) | collective-permute-done | bytes 819232 | tf_op jit(solution)/shard_map/ppermute | solution.py:234
  777.1 4.6 fusion.3
  782.2 39.1 %y.1 = bf16[4096,640]{1,0:T(8,128)(2,1)} custom-call(bf16[4096,5120]{1,0:T(8,128)(2,1)} %get-tuple-element.26.a_ref, bf16[5120,640]{1,0:T(8,128)(2,1)} %constant_dynamic-update-slice_fusion.4.w_ref.wo_ref), custom_call_target="tpu_custom_call" | custom-call | flops 26843545600 | bytes 48496640 | tf_op jit(solution)/shard_map/y/pallas_call | solution.py:125
  833.6 13.9 %collective-permute-done.41 = f32[160,1280]{1,0:T(8,128)S(1)} collective-permute-done((f32[160,1280]{1,0:T(8,128)S(1)}, f32[160,1280]{1,0:T(8,128)S(1)}, u32[]{:S(2)}, u32[]{:S(2)}) %collective-permute-start.41) | collective-permute-done | bytes 819232 | tf_op jit(solution)/shard_map/ppermute | solution.py:240
  847.6 17.5 %collective-permute-done.43 = f32[160,1280]{1,0:T(8,128)S(1)} collective-permute-done((f32[160,1280]{1,0:T(8,128)S(1)}, f32[160,1280]{1,0:T(8,128)S(1)}, u32[]{:S(2)}, u32[]{:S(2)}) %collective-permute-start.43) | collective-permute-done | bytes 819232 | tf_op jit(solution)/shard_map/ppermute | solution.py:240
  865.2 15.4 %collective-permute-done.45 = f32[160,1280]{1,0:T(8,128)S(1)} collective-permute-done((f32[160,1280]{1,0:T(8,128)S(1)}, f32[160,1280]{1,0:T(8,128)S(1)}, u32[]{:S(2)}, u32[]{:S(2)}) %collective-permute-start.45) | collective-permute-done | bytes 819232 | tf_op jit(solution)/shard_map/ppermute | solution.py:240
  880.9 3.1 copy.27
  (135 shorter events, 69.6 us)
Async XLA Ops:
  0.6 39.3 %collective-permute-start.2 = (bf16[320,2560]{1,0:T(8,128)(2,1)}, bf16[320,2560]{1,0:T(8,128)(2,1)}, u32[]{:S(2)}, u32[]{:S(2)}) collective-permute-start(bf16[320,2560]{1,0:T(8,128)(2,1)} %param.5), channel_id=1, source_target_pairs={{0,2},{1,3},{2,0},{3,1},{4,6},{5,7},{6,4},{7,5},{8,10},{9,11},{10,... | collective-permute-start | bytes 4915208 | tf_op jit(solution)/shard_map/ppermute | solution.py:234
  6.0 21.3 %collective-permute-start.4 = (bf16[160,2560]{1,0:T(8,128)(2,1)}, bf16[160,2560]{1,0:T(8,128)(2,1)S(1)}, u32[]{:S(2)}, u32[]{:S(2)}) collective-permute-start(bf16[160,2560]{1,0:T(8,128)(2,1)} %constant_dynamic-slice_fusion.1), channel_id=1, source_target_pairs={{0,4},{4,0},{1,5},{5,1},{2,6},{6,2},{3,7},{7,3},{8,12},{12,8},{9,1... | collective-permute-start | bytes 2457608 | tf_op jit(solution)/shard_map/ppermute | solution.py:237
  7.5 100.9 %collective-permute-start.1 = (bf16[320,2560]{1,0:T(8,128)(2,1)}, bf16[320,2560]{1,0:T(8,128)(2,1)}, u32[]{:S(2)}, u32[]{:S(2)}) collective-permute-start(bf16[320,2560]{1,0:T(8,128)(2,1)} %param.5), channel_id=1, source_target_pairs={{0,1},{1,0},{2,3},{3,2},{4,5},{5,4},{6,7},{7,6},{8,9},{9,8},{10,11... | collective-permute-start | bytes 4915208 | tf_op jit(solution)/shard_map/ppermute | solution.py:231
  20.3 142.8 %collective-permute-start.11 = (bf16[1024,640]{0,1:T(8,128)(2,1)}, bf16[1024,640]{0,1:T(8,128)(2,1)S(1)}, u32[]{:S(2)}, u32[]{:S(2)}) collective-permute-start(bf16[1024,640]{0,1:T(8,128)(2,1)} %get-tuple-element.52), channel_id=1, source_target_pairs={{0,4},{4,0},{1,5},{5,1},{2,6},{6,2},{3,7},{7,3},{8,12},{12,8},{9,1... | collective-permute-start | bytes 3932168 | tf_op jit(solution)/shard_map/ppermute | solution.py:237
  22.9 48.7 %collective-permute-start.16 = (bf16[640,640]{1,0:T(8,128)(2,1)}, bf16[640,640]{1,0:T(8,128)(2,1)}, u32[]{:S(2)}, u32[]{:S(2)}) collective-permute-start(bf16[640,640]{1,0:T(8,128)(2,1)} %constant_dynamic-slice_fusion), channel_id=1, source_target_pairs={{0,4},{4,0},{1,5},{5,1},{2,6},{6,2},{3,7},{7,3},{8,12},{12,8},{9,1... | collective-permute-start | bytes 2457608 | tf_op jit(solution)/shard_map/ppermute | solution.py:237
  24.5 20.7 %slice-start.2 = ((s8[5242880]{0:T(1024)(128)(4,1)}), s8[1048576]{0:T(1024)(128)(4,1)S(1)}, s32[]{:S(2)}) async-start(s8[5242880]{0:T(1024)(128)(4,1)} %bitcast.33), calls=%async_computation.2 | async-start | bytes 2097152
  24.5 20.7 %slice-start.3 = ((s8[5242880]{0:T(1024)(128)(4,1)}), s8[4194304]{0:T(1024)(128)(4,1)S(1)}, s32[]{:S(2)}) async-start(s8[5242880]{0:T(1024)(128)(4,1)} %bitcast.33), calls=%async_computation.3 | async-start | bytes 8388608
  27.3 81.9 %collective-permute-start.5 = (bf16[160,2560]{1,0:T(8,128)(2,1)S(1)}, bf16[160,2560]{1,0:T(8,128)(2,1)}, u32[]{:S(2)}, u32[]{:S(2)}) collective-permute-start(bf16[160,2560]{1,0:T(8,128)(2,1)S(1)} %collective-permute-done.4), channel_id=1, source_target_pairs={{0,8},{8,0},{1,9},{9,1},{2,10},{10,2},{3,11},{11,3},{4,12},{12,4},... | collective-permute-start | bytes 2457608 | tf_op jit(solution)/shard_map/ppermute | solution.py:240
  40.0 73.8 %collective-permute-start.3 = (bf16[320,2560]{1,0:T(8,128)(2,1)}, bf16[320,2560]{1,0:T(8,128)(2,1)}, u32[]{:S(2)}, u32[]{:S(2)}) collective-permute-start(bf16[320,2560]{1,0:T(8,128)(2,1)} %collective-permute-done.2), channel_id=1, source_target_pairs={{0,1},{1,0},{2,3},{3,2},{4,5},{5,4},{6,7},{7,6},{8,9},{9,8},{10,11... | collective-permute-start | bytes 4915208 | tf_op jit(solution)/shard_map/ppermute | solution.py:231
  71.6 40.1 %collective-permute-start.17 = (bf16[640,640]{1,0:T(8,128)(2,1)}, bf16[640,640]{1,0:T(8,128)(2,1)S(1)}, u32[]{:S(2)}, u32[]{:S(2)}) collective-permute-start(bf16[640,640]{1,0:T(8,128)(2,1)} %collective-permute-done.16), channel_id=1, source_target_pairs={{0,8},{8,0},{1,9},{9,1},{2,10},{10,2},{3,11},{11,3},{4,12},{12,4},... | collective-permute-start | bytes 2457608 | tf_op jit(solution)/shard_map/ppermute | solution.py:240
  93.6 14.9 %copy-start.10 = (bf16[1024,640]{0,1:T(8,128)(2,1)S(1)}, bf16[1024,640]{0,1:T(8,128)(2,1)}, u32[]{:S(2)}) copy-start(bf16[1024,640]{0,1:T(8,128)(2,1)} %get-tuple-element.53) | copy-start | bytes 3932164
  93.6 15.6 %copy-start.9 = (bf16[1024,640]{0,1:T(8,128)(2,1)S(1)}, bf16[1024,640]{0,1:T(8,128)(2,1)}, u32[]{:S(2)}) copy-start(bf16[1024,640]{0,1:T(8,128)(2,1)} %get-tuple-element.54) | copy-start | bytes 3932164
  108.4 54.8 %collective-permute-start.10 = (bf16[1024,640]{0,1:T(8,128)(2,1)S(1)}, bf16[1024,640]{0,1:T(8,128)(2,1)}, u32[]{:S(2)}, u32[]{:S(2)}) collective-permute-start(bf16[1024,640]{0,1:T(8,128)(2,1)S(1)} %copy-done.10), channel_id=1, source_target_pairs={{0,4},{4,0},{1,5},{5,1},{2,6},{6,2},{3,7},{7,3},{8,12},{12,8},{9,1... | collective-permute-start | bytes 3932168 | tf_op jit(solution)/shard_map/ppermute | solution.py:237
  109.2 59.2 %collective-permute-start.9 = (bf16[1024,640]{0,1:T(8,128)(2,1)S(1)}, bf16[1024,640]{0,1:T(8,128)(2,1)}, u32[]{:S(2)}, u32[]{:S(2)}) collective-permute-start(bf16[1024,640]{0,1:T(8,128)(2,1)S(1)} %copy-done.9), channel_id=1, source_target_pairs={{0,4},{4,0},{1,5},{5,1},{2,6},{6,2},{3,7},{7,3},{8,12},{12,8},{9,1... | collective-permute-start | bytes 3932168 | tf_op jit(solution)/shard_map/ppermute | solution.py:237
  111.8 82.0 %collective-permute-start = (bf16[1024,640]{0,1:T(8,128)(2,1)}, bf16[1024,640]{0,1:T(8,128)(2,1)}, u32[]{:S(2)}, u32[]{:S(2)}) collective-permute-start(bf16[1024,640]{0,1:T(8,128)(2,1)} %get-tuple-element.55), channel_id=1, source_target_pairs={{0,4},{4,0},{1,5},{5,1},{2,6},{6,2},{3,7},{7,3},{8,12},{12,8},{9,1... | collective-permute-start | bytes 3932168 | tf_op jit(solution)/shard_map/ppermute | solution.py:237
  113.8 86.2 %collective-permute-start.13 = (bf16[1280,640]{1,0:T(8,128)(2,1)}, bf16[1280,640]{1,0:T(8,128)(2,1)}, u32[]{:S(2)}, u32[]{:S(2)}) collective-permute-start(bf16[1280,640]{1,0:T(8,128)(2,1)} %param.6), channel_id=1, source_target_pairs={{0,2},{1,3},{2,0},{3,1},{4,6},{5,7},{6,4},{7,5},{8,10},{9,11},{10,... | collective-permute-start | bytes 4915208 | tf_op jit(solution)/shard_map/ppermute | solution.py:234
  134.2 35.3 %slice-start = ((s8[5242880]{0:T(1024)(128)(4,1)}), s8[4194304]{0:T(1024)(128)(4,1)S(1)}, s32[]{:S(2)}) async-start(s8[5242880]{0:T(1024)(128)(4,1)} %bitcast.27), calls=%async_computation | async-start | bytes 8388608
  149.3 20.2 %slice-start.1 = ((s8[5242880]{0:T(1024)(128)(4,1)}), s8[1048576]{0:T(1024)(128)(4,1)S(1)}, s32[]{:S(2)}) async-start(s8[5242880]{0:T(1024)(128)(4,1)} %bitcast.27), calls=%async_computation.1 | async-start | bytes 2097152
  163.2 39.9 %collective-permute-start.12 = (bf16[1280,640]{1,0:T(8,128)(2,1)}, bf16[1280,640]{1,0:T(8,128)(2,1)}, u32[]{:S(2)}, u32[]{:S(2)}) collective-permute-start(bf16[1280,640]{1,0:T(8,128)(2,1)} %param.6), channel_id=1, source_target_pairs={{0,1},{1,0},{2,3},{3,2},{4,5},{5,4},{6,7},{7,6},{8,9},{9,8},{10,11... | collective-permute-start | bytes 4915208 | tf_op jit(solution)/shard_map/ppermute | solution.py:231
  163.2 39.9 %collective-permute-start.19 = (bf16[1280,640]{1,0:T(8,128)(2,1)}, bf16[1280,640]{1,0:T(8,128)(2,1)}, u32[]{:S(2)}, u32[]{:S(2)}) collective-permute-start(bf16[1280,640]{1,0:T(8,128)(2,1)} %get-tuple-element.64), channel_id=1, source_target_pairs={{0,2},{1,3},{2,0},{3,1},{4,6},{5,7},{6,4},{7,5},{8,10},{9,11},{10,... | collective-permute-start | bytes 4915208 | tf_op jit(solution)/shard_map/ppermute | solution.py:234
  168.3 68.5 %collective-permute-start.7 = (bf16[320,2560]{1,0:T(8,128)(2,1)}, bf16[320,2560]{1,0:T(8,128)(2,1)}, u32[]{:S(2)}, u32[]{:S(2)}) collective-permute-start(bf16[320,2560]{1,0:T(8,128)(2,1)} %get-tuple-element.68), channel_id=1, source_target_pairs={{0,2},{1,3},{2,0},{3,1},{4,6},{5,7},{6,4},{7,5},{8,10},{9,11},{10,... | collective-permute-start | bytes 4915208 | tf_op jit(solution)/shard_map/ppermute | solution.py:234
  196.2 46.1 %collective-permute-start.18 = (bf16[1280,640]{1,0:T(8,128)(2,1)}, bf16[1280,640]{1,0:T(8,128)(2,1)S(1)}, u32[]{:S(2)}, u32[]{:S(2)}) collective-permute-start(bf16[1280,640]{1,0:T(8,128)(2,1)} %get-tuple-element.64), channel_id=1, source_target_pairs={{0,1},{1,0},{2,3},{3,2},{4,5},{5,4},{6,7},{7,6},{8,9},{9,8},{10,11... | collective-permute-start | bytes 4915208 | tf_op jit(solution)/shard_map/ppermute | solution.py:231
  200.0 46.4 %collective-permute-start.14 = (bf16[1280,640]{1,0:T(8,128)(2,1)}, bf16[1280,640]{1,0:T(8,128)(2,1)S(1)}, u32[]{:S(2)}, u32[]{:S(2)}) collective-permute-start(bf16[1280,640]{1,0:T(8,128)(2,1)} %collective-permute-done.13), channel_id=1, source_target_pairs={{0,1},{1,0},{2,3},{3,2},{4,5},{5,4},{6,7},{7,6},{8,9},{9,8},{10,11... | collective-permute-start | bytes 4915208 | tf_op jit(solution)/shard_map/ppermute | solution.py:231
  203.1 46.7 %collective-permute-start.6 = (bf16[320,2560]{1,0:T(8,128)(2,1)}, bf16[320,2560]{1,0:T(8,128)(2,1)S(1)}, u32[]{:S(2)}, u32[]{:S(2)}) collective-permute-start(bf16[320,2560]{1,0:T(8,128)(2,1)} %get-tuple-element.68), channel_id=1, source_target_pairs={{0,1},{1,0},{2,3},{3,2},{4,5},{5,4},{6,7},{7,6},{8,9},{9,8},{10,11... | collective-permute-start | bytes 4915208 | tf_op jit(solution)/shard_map/ppermute | solution.py:231
  203.1 73.6 %collective-permute-start.20 = (bf16[1280,640]{1,0:T(8,128)(2,1)}, bf16[1280,640]{1,0:T(8,128)(2,1)S(1)}, u32[]{:S(2)}, u32[]{:S(2)}) collective-permute-start(bf16[1280,640]{1,0:T(8,128)(2,1)} %collective-permute-done.19), channel_id=1, source_target_pairs={{0,1},{1,0},{2,3},{3,2},{4,5},{5,4},{6,7},{7,6},{8,9},{9,8},{10,11... | collective-permute-start | bytes 4915208 | tf_op jit(solution)/shard_map/ppermute | solution.py:231
  236.9 44.9 %collective-permute-start.8 = (bf16[320,2560]{1,0:T(8,128)(2,1)}, bf16[320,2560]{1,0:T(8,128)(2,1)S(1)}, u32[]{:S(2)}, u32[]{:S(2)}) collective-permute-start(bf16[320,2560]{1,0:T(8,128)(2,1)} %collective-permute-done.7), channel_id=1, source_target_pairs={{0,1},{1,0},{2,3},{3,2},{4,5},{5,4},{6,7},{7,6},{8,9},{9,8},{10,11... | collective-permute-start | bytes 4915208 | tf_op jit(solution)/shard_map/ppermute | solution.py:231
  242.4 182.5 %collective-permute-start.23 = (bf16[1024,640]{1,0:T(8,128)(2,1)}, bf16[1024,640]{1,0:T(8,128)(2,1)}, u32[]{:S(2)}, u32[]{:S(2)}) collective-permute-start(bf16[1024,640]{1,0:T(8,128)(2,1)} %get-tuple-element.48), channel_id=1, source_target_pairs={{0,4},{4,0},{1,5},{5,1},{2,6},{6,2},{3,7},{7,3},{8,12},{12,8},{9,1... | collective-permute-start | bytes 3932168 | tf_op jit(solution)/shard_map/ppermute | solution.py:237
  246.4 203.5 %collective-permute-start.22 = (bf16[1024,640]{1,0:T(8,128)(2,1)}, bf16[1024,640]{1,0:T(8,128)(2,1)}, u32[]{:S(2)}, u32[]{:S(2)}) collective-permute-start(bf16[1024,640]{1,0:T(8,128)(2,1)} %get-tuple-element.49), channel_id=1, source_target_pairs={{0,4},{4,0},{1,5},{5,1},{2,6},{6,2},{3,7},{7,3},{8,12},{12,8},{9,1... | collective-permute-start | bytes 3932168 | tf_op jit(solution)/shard_map/ppermute | solution.py:237
  249.8 225.0 %collective-permute-start.21 = (bf16[1024,640]{1,0:T(8,128)(2,1)}, bf16[1024,640]{1,0:T(8,128)(2,1)}, u32[]{:S(2)}, u32[]{:S(2)}) collective-permute-start(bf16[1024,640]{1,0:T(8,128)(2,1)} %get-tuple-element.50), channel_id=1, source_target_pairs={{0,4},{4,0},{1,5},{5,1},{2,6},{6,2},{3,7},{7,3},{8,12},{12,8},{9,1... | collective-permute-start | bytes 3932168 | tf_op jit(solution)/shard_map/ppermute | solution.py:237
  276.7 223.2 %collective-permute-start.15 = (bf16[1024,640]{1,0:T(8,128)(2,1)}, bf16[1024,640]{1,0:T(8,128)(2,1)}, u32[]{:S(2)}, u32[]{:S(2)}) collective-permute-start(bf16[1024,640]{1,0:T(8,128)(2,1)} %get-tuple-element.51), channel_id=1, source_target_pairs={{0,4},{4,0},{1,5},{5,1},{2,6},{6,2},{3,7},{7,3},{8,12},{12,8},{9,1... | collective-permute-start | bytes 3932168 | tf_op jit(solution)/shard_map/ppermute | solution.py:237
  424.8 215.2 %collective-permute-start.37 = (f32[640,1280]{1,0:T(8,128)}, f32[640,1280]{1,0:T(8,128)}, u32[]{:S(2)}, u32[]{:S(2)}) collective-permute-start(f32[640,1280]{1,0:T(8,128)} %dw2.7), channel_id=1, source_target_pairs={{0,1},{1,0},{2,3},{3,2},{4,5},{5,4},{6,7},{7,6},{8,9},{9,8},{10,11... | collective-permute-start | bytes 9830408 | tf_op jit(solution)/shard_map/ppermute | solution.py:231
  550.9 39.6 %collective-permute-start.25 = (f32[320,1280]{1,0:T(8,128)}, f32[320,1280]{1,0:T(8,128)}, u32[]{:S(2)}, u32[]{:S(2)}) collective-permute-start(f32[320,1280]{1,0:T(8,128)} %get-tuple-element.31), channel_id=1, source_target_pairs={{0,1},{1,0},{2,3},{3,2},{4,5},{5,4},{6,7},{7,6},{8,9},{9,8},{10,11... | collective-permute-start | bytes 4915208 | tf_op jit(solution)/shard_map/ppermute | solution.py:231
  589.9 136.5 %collective-permute-start.36 = (f32[640,1280]{1,0:T(8,128)}, f32[640,1280]{1,0:T(8,128)}, u32[]{:S(2)}, u32[]{:S(2)}) collective-permute-start(f32[640,1280]{1,0:T(8,128)} %dw2.5), channel_id=1, source_target_pairs={{0,1},{1,0},{2,3},{3,2},{4,5},{5,4},{6,7},{7,6},{8,9},{9,8},{10,11... | collective-permute-start | bytes 9830408 | tf_op jit(solution)/shard_map/ppermute | solution.py:231
  590.0 48.0 %collective-permute-start.24 = (f32[320,1280]{1,0:T(8,128)}, f32[320,1280]{1,0:T(8,128)S(1)}, u32[]{:S(2)}, u32[]{:S(2)}) collective-permute-start(f32[320,1280]{1,0:T(8,128)} %get-tuple-element.29), channel_id=1, source_target_pairs={{0,1},{1,0},{2,3},{3,2},{4,5},{5,4},{6,7},{7,6},{8,9},{9,8},{10,11... | collective-permute-start | bytes 4915208 | tf_op jit(solution)/shard_map/ppermute | solution.py:231
  590.4 48.2 %collective-permute-start.30 = (f32[320,1280]{1,0:T(8,128)}, f32[320,1280]{1,0:T(8,128)S(1)}, u32[]{:S(2)}, u32[]{:S(2)}) collective-permute-start(f32[320,1280]{1,0:T(8,128)} %get-tuple-element.33), channel_id=1, source_target_pairs={{0,1},{1,0},{2,3},{3,2},{4,5},{5,4},{6,7},{7,6},{8,9},{9,8},{10,11... | collective-permute-start | bytes 4915208 | tf_op jit(solution)/shard_map/ppermute | solution.py:231
  590.5 43.2 %collective-permute-start.31 = (f32[320,1280]{1,0:T(8,128)}, f32[320,1280]{1,0:T(8,128)}, u32[]{:S(2)}, u32[]{:S(2)}) collective-permute-start(f32[320,1280]{1,0:T(8,128)} %get-tuple-element.35), channel_id=1, source_target_pairs={{0,1},{1,0},{2,3},{3,2},{4,5},{5,4},{6,7},{7,6},{8,9},{9,8},{10,11... | collective-permute-start | bytes 4915208 | tf_op jit(solution)/shard_map/ppermute | solution.py:231
  630.3 4.8 copy-start.8
  633.7 24.1 %collective-permute-start.26 = (f32[320,640]{1,0:T(8,128)}, f32[320,640]{1,0:T(8,128)S(1)}, u32[]{:S(2)}, u32[]{:S(2)}) collective-permute-start(f32[320,640]{1,0:T(8,128)} %get-tuple-element.58), channel_id=1, source_target_pairs={{0,2},{1,3},{2,0},{3,1},{4,6},{5,7},{6,4},{7,5},{8,10},{9,11},{10,... | collective-permute-start | bytes 2457608 | tf_op jit(solution)/shard_map/ppermute | solution.py:234
  638.0 15.1 %copy-start.7 = (f32[320,1280]{1,0:T(8,128)}, f32[320,1280]{1,0:T(8,128)S(1)}, u32[]{:S(2)}) copy-start(f32[320,1280]{1,0:T(8,128)S(1)} %collective-permute-done.24) | copy-start | bytes 4915204
  638.0 34.7 %collective-permute-start.28 = (f32[320,640]{1,0:T(8,128)}, f32[320,640]{1,0:T(8,128)}, u32[]{:S(2)}, u32[]{:S(2)}) collective-permute-start(f32[320,640]{1,0:T(8,128)} %get-tuple-element.59), channel_id=1, source_target_pairs={{0,2},{1,3},{2,0},{3,1},{4,6},{5,7},{6,4},{7,5},{8,10},{9,11},{10,... | collective-permute-start | bytes 2457608 | tf_op jit(solution)/shard_map/ppermute | solution.py:234
  638.6 14.5 %copy-start.5 = (f32[320,1280]{1,0:T(8,128)}, f32[320,1280]{1,0:T(8,128)S(1)}, u32[]{:S(2)}) copy-start(f32[320,1280]{1,0:T(8,128)S(1)} %collective-permute-done.30) | copy-start | bytes 4915204
  638.6 51.6 %collective-permute-start.32 = (f32[320,640]{1,0:T(8,128)}, f32[320,640]{1,0:T(8,128)}, u32[]{:S(2)}, u32[]{:S(2)}) collective-permute-start(f32[320,640]{1,0:T(8,128)} %get-tuple-element.62), channel_id=1, source_target_pairs={{0,2},{1,3},{2,0},{3,1},{4,6},{5,7},{6,4},{7,5},{8,10},{9,11},{10,... | collective-permute-start | bytes 2457608 | tf_op jit(solution)/shard_map/ppermute | solution.py:234
  640.0 67.7 %collective-permute-start.34 = (f32[320,640]{1,0:T(8,128)}, f32[320,640]{1,0:T(8,128)}, u32[]{:S(2)}, u32[]{:S(2)}) collective-permute-start(f32[320,640]{1,0:T(8,128)} %get-tuple-element.63), channel_id=1, source_target_pairs={{0,2},{1,3},{2,0},{3,1},{4,6},{5,7},{6,4},{7,5},{8,10},{9,11},{10,... | collective-permute-start | bytes 2457608 | tf_op jit(solution)/shard_map/ppermute | solution.py:234
  657.8 63.8 %copy-start.11 = (f32[320,640]{1,0:T(8,128)}, f32[320,640]{1,0:T(8,128)S(1)}, u32[]{:S(2)}) copy-start(f32[320,640]{1,0:T(8,128)S(1)} %collective-permute-done.26) | copy-start | bytes 2457604
  657.8 69.0 %collective-permute-start.38 = (f32[160,1280]{1,0:T(8,128)}, f32[160,1280]{1,0:T(8,128)}, u32[]{:S(2)}, u32[]{:S(2)}) collective-permute-start(f32[160,1280]{1,0:T(8,128)} %get-tuple-element.44), channel_id=1, source_target_pairs={{0,2},{1,3},{2,0},{3,1},{4,6},{5,7},{6,4},{7,5},{8,10},{9,11},{10,... | collective-permute-start | bytes 2457608 | tf_op jit(solution)/shard_map/ppermute | solution.py:234
  672.6 70.2 %collective-permute-start.40 = (f32[160,1280]{1,0:T(8,128)}, f32[160,1280]{1,0:T(8,128)}, u32[]{:S(2)}, u32[]{:S(2)}) collective-permute-start(f32[160,1280]{1,0:T(8,128)} %get-tuple-element.47), channel_id=1, source_target_pairs={{0,2},{1,3},{2,0},{3,1},{4,6},{5,7},{6,4},{7,5},{8,10},{9,11},{10,... | collective-permute-start | bytes 2457608 | tf_op jit(solution)/shard_map/ppermute | solution.py:234
  690.2 70.2 %collective-permute-start.42 = (f32[160,1280]{1,0:T(8,128)}, f32[160,1280]{1,0:T(8,128)}, u32[]{:S(2)}, u32[]{:S(2)}) collective-permute-start(f32[160,1280]{1,0:T(8,128)} %get-tuple-element.46), channel_id=1, source_target_pairs={{0,2},{1,3},{2,0},{3,1},{4,6},{5,7},{6,4},{7,5},{8,10},{9,11},{10,... | collective-permute-start | bytes 2457608 | tf_op jit(solution)/shard_map/ppermute | solution.py:234
  707.8 69.3 %collective-permute-start.44 = (f32[160,1280]{1,0:T(8,128)}, f32[160,1280]{1,0:T(8,128)}, u32[]{:S(2)}, u32[]{:S(2)}) collective-permute-start(f32[160,1280]{1,0:T(8,128)} %get-tuple-element.45), channel_id=1, source_target_pairs={{0,2},{1,3},{2,0},{3,1},{4,6},{5,7},{6,4},{7,5},{8,10},{9,11},{10,... | collective-permute-start | bytes 2457608 | tf_op jit(solution)/shard_map/ppermute | solution.py:234
  709.2 12.4 %copy-start.3 = (f32[320,1280]{1,0:T(8,128)S(1)}, f32[320,1280]{1,0:T(8,128)}, u32[]{:S(2)}) copy-start(f32[320,1280]{1,0:T(8,128)} %get-tuple-element.28) | copy-start | bytes 4915204
  721.6 2.4 copy-start.4
  721.6 2.9 copy-start.6
  724.5 52.6 %copy-start = (f32[640,1280]{1,0:T(8,128)S(1)}, f32[640,1280]{1,0:T(8,128)}, u32[]{:S(2)}) copy-start(f32[640,1280]{1,0:T(8,128)} %dw2.4) | copy-start | bytes 9830404
  726.3 95.0 %collective-permute-start.27 = (f32[320,640]{1,0:T(8,128)S(1)}, f32[320,640]{1,0:T(8,128)}, u32[]{:S(2)}, u32[]{:S(2)}) collective-permute-start(f32[320,640]{1,0:T(8,128)S(1)} %get-tuple-element.56), channel_id=1, source_target_pairs={{0,8},{8,0},{1,9},{9,1},{2,10},{10,2},{3,11},{11,3},{4,12},{12,4},... | collective-permute-start | bytes 2457608 | tf_op jit(solution)/shard_map/ppermute | solution.py:240
  726.8 95.7 %collective-permute-start.29 = (f32[320,640]{1,0:T(8,128)S(1)}, f32[320,640]{1,0:T(8,128)}, u32[]{:S(2)}, u32[]{:S(2)}) collective-permute-start(f32[320,640]{1,0:T(8,128)S(1)} %get-tuple-element.57), channel_id=1, source_target_pairs={{0,8},{8,0},{1,9},{9,1},{2,10},{10,2},{3,11},{11,3},{4,12},{12,4},... | collective-permute-start | bytes 2457608 | tf_op jit(solution)/shard_map/ppermute | solution.py:240
  742.9 81.0 %collective-permute-start.33 = (f32[320,640]{1,0:T(8,128)S(1)}, f32[320,640]{1,0:T(8,128)}, u32[]{:S(2)}, u32[]{:S(2)}) collective-permute-start(f32[320,640]{1,0:T(8,128)S(1)} %get-tuple-element.60), channel_id=1, source_target_pairs={{0,8},{8,0},{1,9},{9,1},{2,10},{10,2},{3,11},{11,3},{4,12},{12,4},... | collective-permute-start | bytes 2457608 | tf_op jit(solution)/shard_map/ppermute | solution.py:240
  760.4 64.7 %collective-permute-start.35 = (f32[320,640]{1,0:T(8,128)S(1)}, f32[320,640]{1,0:T(8,128)}, u32[]{:S(2)}, u32[]{:S(2)}) collective-permute-start(f32[320,640]{1,0:T(8,128)S(1)} %get-tuple-element.61), channel_id=1, source_target_pairs={{0,8},{8,0},{1,9},{9,1},{2,10},{10,2},{3,11},{11,3},{4,12},{12,4},... | collective-permute-start | bytes 2457608 | tf_op jit(solution)/shard_map/ppermute | solution.py:240
  781.7 50.4 %collective-permute-start.39 = (f32[160,1280]{1,0:T(8,128)}, f32[160,1280]{1,0:T(8,128)}, u32[]{:S(2)}, u32[]{:S(2)}) collective-permute-start(f32[160,1280]{1,0:T(8,128)} %get-tuple-element.40), channel_id=1, source_target_pairs={{0,8},{8,0},{1,9},{9,1},{2,10},{10,2},{3,11},{11,3},{4,12},{12,4},... | collective-permute-start | bytes 2457608 | tf_op jit(solution)/shard_map/ppermute | solution.py:240
  822.6 3.8 copy-start.2
  826.4 3.7 copy-start.1
  826.4 21.1 %collective-permute-start.41 = (f32[160,1280]{1,0:T(8,128)S(1)}, f32[160,1280]{1,0:T(8,128)S(1)}, u32[]{:S(2)}, u32[]{:S(2)}) collective-permute-start(f32[160,1280]{1,0:T(8,128)S(1)} %copy-done.2), channel_id=1, source_target_pairs={{0,8},{8,0},{1,9},{9,1},{2,10},{10,2},{3,11},{11,3},{4,12},{12,4},... | collective-permute-start | bytes 2457608 | tf_op jit(solution)/shard_map/ppermute | solution.py:240
  830.1 35.0 %collective-permute-start.43 = (f32[160,1280]{1,0:T(8,128)S(1)}, f32[160,1280]{1,0:T(8,128)S(1)}, u32[]{:S(2)}, u32[]{:S(2)}) collective-permute-start(f32[160,1280]{1,0:T(8,128)S(1)} %copy-done.1), channel_id=1, source_target_pairs={{0,8},{8,0},{1,9},{9,1},{2,10},{10,2},{3,11},{11,3},{4,12},{12,4},... | collective-permute-start | bytes 2457608 | tf_op jit(solution)/shard_map/ppermute | solution.py:240
  830.6 50.1 %collective-permute-start.45 = (f32[160,1280]{1,0:T(8,128)S(1)}, f32[160,1280]{1,0:T(8,128)S(1)}, u32[]{:S(2)}, u32[]{:S(2)}) collective-permute-start(f32[160,1280]{1,0:T(8,128)S(1)} %get-tuple-element.41), channel_id=1, source_target_pairs={{0,8},{8,0},{1,9},{9,1},{2,10},{10,2},{3,11},{11,3},{4,12},{12,4},... | collective-permute-start | bytes 2457608 | tf_op jit(solution)/shard_map/ppermute | solution.py:240

commit v2 on v1

v2 whole, which is shorter than its diff:
```python
import jax
import jax.numpy as jnp
from jax import lax
from jax.experimental import pallas as pl
from jax.experimental.pallas import tpu as pltpu
from jax.sharding import PartitionSpec as P


BF16, F32 = jnp.bfloat16, jnp.float32
VMEM_LIMIT = 60 * 1024 * 1024
SQRT_2_OVER_PI = 0.7978845608028654
CUBIC = 0.044715
NCHUNK = 4
NFIRST = 2
NPIECE2 = 2
NPIECE1 = 4
NOUT = 2
SUB = 512
MESH = pl.DeviceIdType.MESH
LAST_LAST = (((1,), (1,)), ((), ()))


def dot(a, b):
    return jnp.dot(a, b, preferred_element_type=F32)


def dot_t(a, b):
    return lax.dot_general(a, b, LAST_LAST, preferred_element_type=F32)


def cost(flops, nbytes, trans=0):
    return pl.CostEstimate(flops=flops, bytes_accessed=nbytes, transcendentals=trans)


def params():
    return pltpu.CompilerParams(vmem_limit_bytes=VMEM_LIMIT)


def gather_body(w1_ref, w2_ref, tok_ref, w1, w2, tok_oth, send, recv, local):
    col, row, depth = lax.axis_index("col"), lax.axis_index("row"), lax.axis_index("depth")
    x, core = row // 2, row % 2
    to_core = {"row": 2 * x + (1 - core)}
    to_x = {"row": 2 * (1 - x) + core}
    to_col = {"col": 1 - col}
    to_depth = {"depth": 1 - depth}

    barrier = pltpu.get_barrier_semaphore()
    for dev in (to_core, to_x, to_col, to_depth):
        pl.semaphore_signal(barrier, inc=1, device_id=dev, device_id_type=MESH)
    pl.semaphore_wait(barrier, 4)

    def place(which, bx, bcol, at_col, half=None):
        ref = (w1_ref, w2_ref)[which]
        n, m = ref.shape
        side = (bx + at_col) % 2 if which == 0 else (bcol + at_col) % 2
        if which == 0:
            r0, c0 = side * (2 * n) + core * n, bcol * m
        else:
            r0, c0 = (2 * bx + core) * n, side * m
        if half is not None:
            r0, n = r0 + half * (n // 2), n // 2
        return (w1, w2)[which].at[pl.ds(pl.multiple_of(r0, 32), n), pl.ds(pl.multiple_of(c0, 128), m)]

    made = []

    def start(src, dst, dev):
        i = len(made)
        cp = pltpu.make_async_remote_copy(src_ref=src, dst_ref=dst, send_sem=send.at[i], recv_sem=recv.at[i],
                                          device_id=dev, device_id_type=MESH)
        cp.start()
        made.append(cp)
        return cp

    def forward(piece, dev):
        return start(piece, piece, dev)

    def half_of(ref):
        n = ref.shape[0] // 2
        return ref.at[pl.ds(pl.multiple_of(depth * n, 32), n), :]

    late = []

    def to_partner(piece):
        late.append(forward(piece, to_core))

    other = 1 - col
    col1 = start(half_of(w1_ref), place(0, x, col, other, depth), to_col)
    x1 = start(w1_ref, place(0, x, col, col), to_x)
    col2 = start(half_of(w2_ref), place(1, x, col, other, depth), to_col)
    first = tok_oth.shape[0]
    late.append(start(tok_ref.at[pl.ds(0, first), :], tok_oth, to_col))
    late.append(start(w1_ref, place(0, x, col, col), to_core))
    late.append(start(w2_ref, place(1, x, col, col), to_core))
    keep = [pltpu.make_async_copy(w1_ref, place(0, x, col, col), local.at[0]),
            pltpu.make_async_copy(w2_ref, place(1, x, col, col), local.at[1])]
    for cp in keep:
        cp.start()

    def oth(which, bx, half):
        return place(which, bx, other, col, half)

    col1.wait_recv()
    z1 = forward(oth(0, x, depth), to_depth)
    x1h = forward(oth(0, x, depth), to_x)
    to_partner(oth(0, x, depth))
    x2 = start(half_of(w2_ref), place(1, x, col, col, depth), to_x)
    col2.wait_recv()
    z2 = forward(oth(1, x, depth), to_depth)
    x2h = forward(oth(1, x, depth), to_x)
    to_partner(oth(1, x, depth))
    z1.wait_recv()
    to_partner(oth(0, x, 1 - depth))
    x1.wait_recv()
    to_partner(place(0, 1 - x, col, col))
    x1h.wait_recv()
    z1d = forward(oth(0, 1 - x, depth), to_depth)
    to_partner(oth(0, 1 - x, depth))
    z2.wait_recv()
    to_partner(oth(1, x, 1 - depth))
    x2.wait_recv()
    z2o = forward(place(1, 1 - x, col, col, depth), to_depth)
    to_partner(place(1, 1 - x, col, col, depth))
    z1d.wait_recv()
    to_partner(oth(0, 1 - x, 1 - depth))
    x2h.wait_recv()
    z2d = forward(oth(1, 1 - x, depth), to_depth)
    to_partner(oth(1, 1 - x, depth))
    z2o.wait_recv()
    to_partner(place(1, 1 - x, col, col, 1 - depth))
    z2d.wait_recv()
    to_partner(oth(1, 1 - x, 1 - depth))
    for cp in late:
        cp.wait_recv()
    for cp in made:
        cp.wait_send()
    for cp in keep:
        cp.wait()


NCOPY = 25


def gather_kernel(up, down, tok, first):
    return pl.pallas_call(
        gather_body,
        in_specs=[pl.BlockSpec(memory_space=pl.ANY)] * 3,
        out_specs=[pl.BlockSpec(memory_space=pl.ANY)] * 3,
        out_shape=[jax.ShapeDtypeStruct((4 * up.shape[0], 2 * up.shape[1]), BF16),
                   jax.ShapeDtypeStruct((4 * down.shape[0], 2 * down.shape[1]), BF16),
                   jax.ShapeDtypeStruct((first, tok.shape[1]), BF16)],
        scratch_shapes=[pltpu.SemaphoreType.DMA((NCOPY,)), pltpu.SemaphoreType.DMA((NCOPY,)), pltpu.SemaphoreType.DMA((2,))],
        compiler_params=pltpu.CompilerParams(collective_id=0, has_side_effects=True),
        cost_estimate=cost(0, 300_000_000),
        name="gather",
    )(up, down, tok)


ANY = pl.BlockSpec(memory_space=pl.ANY)


def up_body(xo_ref, xt_ref, w_ref, *rest):
    a_ref, d_ref, x_ref = rest[-3:]
    hh = xo_ref.shape[1]

    @pl.when(pl.program_id(0) == 0)
    def _():
        x_ref[:, :hh] = xo_ref[...]
        x_ref[:, hh:] = xt_ref[...]

    rows = xo_ref.shape[0]
    for i in range(rows // SUB):
        sl = pl.ds(i * SUB, SUB)
        u = dot(x_ref[sl, :], w_ref[...])
        u2 = u * u
        t = jnp.tanh(u * (SQRT_2_OVER_PI + (SQRT_2_OVER_PI * CUBIC) * u2))
        h = 0.5 + 0.5 * t
        a_ref[sl, :] = (u * h).astype(BF16)
        slope = SQRT_2_OVER_PI + (3.0 * SQRT_2_OVER_PI * CUBIC) * u2
        d_ref[sl, :] = h + ((1.0 - t * t) * (0.5 * u)) * slope


def up_kernel(x_own, x_oth, at, w1, rows, chunk, bufs, bn=512):
    tokens, hh = x_own.shape
    f = w1.shape[1]
    in_specs = [
        pl.BlockSpec((rows, hh), lambda j: (chunk, 0)),
        pl.BlockSpec((rows, hh), lambda j: (at, 0)),
        pl.BlockSpec((2 * hh, bn), lambda j: (0, j)),
    ]
    out_spec = pl.BlockSpec((rows, bn), lambda j: (chunk, j))
    args = [x_own, x_oth, w1]
    aliases = {}
    if bufs is not None:
        in_specs += [ANY] * 2
        args += list(bufs)
        aliases = {3: 0, 4: 1}
    return pl.pallas_call(
        up_body,
        grid=(f // bn,),
        in_specs=in_specs,
        out_specs=[out_spec, out_spec],
        scratch_shapes=[pltpu.VMEM((rows, 2 * hh), BF16)],
        out_shape=[jax.ShapeDtypeStruct((tokens, f), BF16), jax.ShapeDtypeStruct((tokens, f), F32)],
        input_output_aliases=aliases,
        compiler_params=params(),
        cost_estimate=cost(2 * rows * 2 * hh * f, rows * f * 6 + 2 * hh * f * 2, rows * f),
        name="up",
    )(*args)


def du_body(go_ref, gt_ref, w_ref, d_ref, *rest):
    u_ref, g_ref = rest[-2:]
    hh = go_ref.shape[1]

    @pl.when(pl.program_id(0) == 0)
    def _():
        g_ref[:, :hh] = go_ref[...]
        g_ref[:, hh:] = gt_ref[...]

    rows = go_ref.shape[0]
    for i in range(rows // SUB):
        sl = pl.ds(i * SUB, SUB)
        u_ref[sl, :] = (dot_t(g_ref[sl, :], w_ref[...]) * d_ref[sl, :]).astype(BF16)


def du_kernel(g_own, g_oth, at, w2, d, rows, chunk, buf, after, bn=512):
    tokens, hh = g_own.shape
    f = w2.shape[0]
    in_specs = [
        pl.BlockSpec((rows, hh), lambda j: (chunk, 0)),
        pl.BlockSpec((rows, hh), lambda j: (at, 0)),
        pl.BlockSpec((bn, 2 * hh), lambda j: (j, 0)),
        pl.BlockSpec((rows, bn), lambda j: (chunk, j)),
        ANY,
    ]
    args = [g_own, g_oth, w2, d, after if buf is None else buf]
    return pl.pallas_call(
        du_body,
        grid=(f // bn,),
        in_specs=in_specs,
        out_specs=pl.BlockSpec((rows, bn), lambda j: (chunk, j)),
        scratch_shapes=[pltpu.VMEM((rows, 2 * hh), BF16)],
        out_shape=jax.ShapeDtypeStruct((tokens, f), BF16),
        input_output_aliases={} if buf is None else {4: 0},
        compiler_params=params(),
        cost_estimate=cost(2 * rows * 2 * hh * f, rows * f * 6 + 2 * hh * f * 2),
        name="du",
    )(*args)


def y_body(a_ref, w_ref, dep_ref, o_ref):
    o_ref[...] = dot(a_ref[...], w_ref[...]).astype(BF16)


def dx_body(u_ref, w_ref, dep_ref, o_ref):
    o_ref[...] = dot_t(u_ref[...], w_ref[...]).astype(BF16)


def out_kernel(body, a, w, w_shape, hh, part, nparts, after, chained, bm=512):
    tokens, f = a.shape
    steps = tokens // nparts // bm
    return pl.pallas_call(
        body,
        grid=(steps,),
        in_specs=[pl.BlockSpec((bm, f), lambda i: (part * steps + i, 0)), pl.BlockSpec(w_shape, lambda i: (0, 0)), ANY],
        out_specs=pl.BlockSpec((bm, hh), lambda i: (part * steps + i, 0)),
        out_shape=jax.ShapeDtypeStruct((tokens, hh), BF16),
        input_output_aliases={2: 0} if chained else {},
        compiler_params=params(),
        cost_estimate=cost(2 * tokens * f * hh // nparts, tokens * f * 2 // nparts + f * hh * 2),
    )(a, w, after)


def dw2_body(s_ref, g_ref, a_ref, dep_ref, o_ref):
    o_ref[...] = dot(g_ref[...], a_ref[...])


def dw2_kernel(idx, g_t, a, width, after, bn=512):
    n, tokens = g_t.shape
    steps = width // bn
    return pl.pallas_call(
        dw2_body,
        grid_spec=pltpu.PrefetchScalarGridSpec(
            num_scalar_prefetch=1,
            grid=(steps,),
            in_specs=[
                pl.BlockSpec((n, tokens), lambda j, s: (0, 0)),
                pl.BlockSpec((tokens, bn), lambda j, s: (0, s[0] * steps + j)),
                ANY,
            ],
            out_specs=pl.BlockSpec((n, bn), lambda j, s: (0, j))),
        out_shape=jax.ShapeDtypeStruct((n, width), F32),
        compiler_params=params(),
        cost_estimate=cost(2 * tokens * n * width, tokens * (n + width) * 2 + n * width * 4),
        name="dw2",
    )(idx, g_t, a, after)


def dw1_body(s_ref, x_ref, u_ref, dep_ref, mine_ref, theirs_ref):
    r = dot(x_ref[...], u_ref[...])
    half = r.shape[0] // 2

    @pl.when(s_ref[2] == 0)
    def _():
        mine_ref[...] = r[:half]
        theirs_ref[...] = r[half:]

    @pl.when(s_ref[2] != 0)
    def _():
        mine_ref[...] = r[half:]
        theirs_ref[...] = r[:half]


def dw1_kernel(s, x_t, du, width, after, bn=512):
    hrows, tokens = x_t.shape
    half = hrows // 2
    steps = width // bn
    out_spec = pl.BlockSpec((half // 2, bn), lambda j, s: (0, j))
    shape = jax.ShapeDtypeStruct((half // 2, width), F32)
    return pl.pallas_call(
        dw1_body,
        grid_spec=pltpu.PrefetchScalarGridSpec(
            num_scalar_prefetch=1,
            grid=(steps,),
            in_specs=[
                pl.BlockSpec((half, tokens), lambda j, s: (s[0], 0)),
                pl.BlockSpec((tokens, bn), lambda j, s: (0, s[1] * steps + j)),
                ANY,
            ],
            out_specs=[out_spec, out_spec]),
        out_shape=[shape, shape],
        compiler_params=params(),
        cost_estimate=cost(2 * tokens * half * width, tokens * (half + width) * 2 + half * width * 4),
        name="dw1",
    )(s, x_t, du, after)


def solution(mesh):
    nx = mesh.shape["row"] // 2
    act_spec = P(("depth", "row"), "col")
    weight_spec = P("row", "col")
    pair = [(0, 1), (1, 0)]
    core_pair = [(r, r ^ 1) for r in range(2 * nx)]
    x_pair = [(r, r ^ 2) for r in range(2 * nx)]

    def over_core(v):
        return lax.ppermute(v, "row", core_pair)

    def over_x(v):
        return lax.ppermute(v, "row", x_pair)

    def over_col(v):
        return lax.ppermute(v, "col", pair)

    def over_depth(v):
        return lax.ppermute(v, "depth", pair)

    def body(tok, up, down, grad):
        col = lax.axis_index("col")
        row = lax.axis_index("row")
        x, core = row // 2, row % 2
        tokens, hh = tok.shape
        rows = tokens // NCHUNK
        fh = up.shape[1]

        w1, w2, tok_first = gather_kernel(up, down, tok, NFIRST * rows)
        tok_oth = [(tok_first, i) for i in range(NFIRST)]
        for i in range(NFIRST, NCHUNK):
            tok_oth.append((over_col(tok[i * rows:(i + 1) * rows]), 0))
        grad_oth = [(over_col(grad[i * rows:(i + 1) * rows]), 0) for i in range(NCHUNK)]

        grad_t = grad.T
        x_t = jnp.concatenate([tok.T, jnp.concatenate([tok_first.T] + [t.T for t, _ in tok_oth[NFIRST:]], axis=1)], axis=0)

        bufs = None
        for i in range(NCHUNK):
            bufs = up_kernel(tok, *tok_oth[i], w1, rows, i, bufs)
        a, d = bufs

        away = dw2_kernel(jnp.stack([1 - x]), grad_t, a, fh, d)
        here = dw2_kernel(jnp.stack([x]), grad_t, a, fh, away)
        fb = fh // 2

        def of_core(v, c, r0, n):
            return lax.dynamic_slice(v, (r0, c * fb), (n, fb))

        got_away = over_core(of_core(away, 1 - core, 0, hh))
        got_here = over_core(of_core(here, 1 - core, 0, hh))
        pieces = []
        n = hh // NPIECE2
        for p in range(NPIECE2):
            sl = slice(p * n, (p + 1) * n)
            out = of_core(away, core, p * n, n) + got_away[sl]
            came = over_x(out)
            layer = (of_core(here, core, p * n, n) + got_here[sl]) + came
            pieces.append((layer + over_depth(layer)).T)
        dw_down = jnp.concatenate(pieces, axis=1)

        du = None
        for i in range(NCHUNK):
            du = du_kernel(grad, *grad_oth[i], w2, d, rows, i, du, here)

        away = dw1_kernel(jnp.stack([(1 - x + col) % 2, col, core]), x_t, du, fh, du)
        here = dw1_kernel(jnp.stack([(x + col) % 2, col, core]), x_t, du, fh, away[0])
        got_away = over_core(away[1])
        got_here = over_core(here[1])
        cols = []
        w = fh // NPIECE1
        for p in range(NPIECE1):
            sl = slice(p * w, (p + 1) * w)
            out = away[0][:, sl] + got_away[:, sl]
            came = over_x(out)
            layer = (here[0][:, sl] + got_here[:, sl]) + came
            cols.append(layer + over_depth(layer))
        dw_up = jnp.concatenate(cols, axis=1)

        dep = here[0]
        out_blk = dx_blk = None
        for p in range(NOUT):
            out_blk = out_kernel(y_body, a, w2, (w2.shape[0], hh), hh, p, NOUT, dep if p == 0 else out_blk, p > 0)
        for p in range(NOUT):
            dx_blk = out_kernel(dx_body, du, w1, (hh, w1.shape[1]), hh, p, NOUT, out_blk if p == 0 else dx_blk, p > 0)
        return out_blk, dx_blk, dw_up, dw_down

    return jax.shard_map(body, mesh=mesh, in_specs=(act_spec, weight_spec, weight_spec, act_spec),
                         out_specs=(act_spec, act_spec, weight_spec, weight_spec), check_vma=False)
```

time: 898 us -> 866 us (0.964)
  Pallas kernels: 399 us -> 619 us
  local copies, waits for them, and re-layouts: 182 us -> 42 us
  waiting for transfers between devices: 226 us -> 122 us
  starting transfers between devices: 40.6 us -> 22 us
  other arithmetic: 35.9 us -> 50.3 us
    pallas_call x6 -> x9, Pallas kernels: 197 us -> 445 us  [the longest x1 245 us: gather_kernel(): pl.pallas_call(gather_body, in_specs=[pl.BlockSpec(memory_space=pl.ANY)]...]
    dynamic_update_slice x19 -> x0, local copies, waits for them, and re-layouts: 124 us -> none  [the longest x4 58.5 us: body(): w1 = lax.dynamic_update_slice(w1, b, (r * up.shape[0], col * fh))]
    ppermute x12 -> x6, waiting for transfers between devices: 135 us -> 77.8 us  [over_x(): return lax.ppermute(v, 'row', x_pair)]
    ppermute x10 -> x6, waiting for transfers between devices: 43.9 us -> 0.02 us  [over_col(): return lax.ppermute(v, 'col', pair)]
    concatenate x2 -> x1, other arithmetic: 3.9 us -> 21 us  [body(): jnp.concatenate([tok.T, jnp.concatenate([tok_first.T] + [t.T for t, _ in...]
    broadcast_in_dim x2 -> x0, local copies, waits for them, and re-layouts: 11.5 us -> none  [the longest x1 6.39 us: body(): w1 = jnp.zeros((4 * up.shape[0], 2 * fh), BF16)]
    pallas_call x4 -> x2, Pallas kernels: 52.3 us -> 40.8 us  [dw1_kernel(): pl.pallas_call(dw1_body, grid_spec=pltpu.PrefetchScalarGridSpec(num_scala...]
    pallas_call x4 -> x2, Pallas kernels: 49.3 us -> 39.1 us  [dw2_kernel(): pl.pallas_call(dw2_body, grid_spec=pltpu.PrefetchScalarGridSpec(num_scala...]
  transfers between devices with their start and end apart: 46 -> 22, of which waited for: 15 -> 7; matrix products, arithmetic and copies ran while one was open for 24% -> 9% of each run, Pallas kernels for 45% -> 72%
where the time goes in v2:
time: 866 us; the launch traced here: 856 us
  Pallas kernels  619 us (71%)
  waiting for transfers between devices  122 us (14%)
  other arithmetic  50.3 us (6%)
  local copies, waits for them, and re-layouts  42 us (5%)
  starting transfers between devices  22 us (3%)
    pallas_call x1, Pallas kernels, gather_kernel(): pl.pallas_call(gather_body, in_specs=[pl.BlockSpec(memory_space=pl.ANY)]...  245 us
    pallas_call x4, Pallas kernels, up_kernel(): pl.pallas_call(up_body, grid=(f // bn,), in_specs=in_specs, out_specs=[ou...  111 us
    pallas_call x4, Pallas kernels, du_kernel(): pl.pallas_call(du_body, grid=(f // bn,), in_specs=in_specs, out_specs=pl....  94 us
    pallas_call x4, Pallas kernels, out_kernel(): pl.pallas_call(body, grid=(steps,), in_specs=[pl.BlockSpec((bm, f), lambd...  89.4 us
    ppermute x6, waiting for transfers between devices, over_x(): return lax.ppermute(v, 'row', x_pair)  77.8 us
    ppermute x6, waiting for transfers between devices, over_depth(): return lax.ppermute(v, 'depth', pair)  44 us
    pallas_call x2, Pallas kernels, dw1_kernel(): pl.pallas_call(dw1_body, grid_spec=pltpu.PrefetchScalarGridSpec(num_scala...  40.8 us
    pallas_call x2, Pallas kernels, dw2_kernel(): pl.pallas_call(dw2_body, grid_spec=pltpu.PrefetchScalarGridSpec(num_scala...  39.1 us
  transfers between devices with their start and end apart: 22, of which 7 were waited for; matrix products, arithmetic and copies ran while one was open for 9% of the time, Pallas kernels for 72%

profile of v2, /device:TPU:0, one launch (start us, length us, event | category | flops | bytes accessed | tf_op | source)
XLA Modules:
  0.0 856.2 jit_solution(1065463621052474197)
XLA Ops:
  0.6 7.9 copy.19
  8.5 3.6 fusion.7
  12.1 3.2 collective-permute-start.1
  15.3 2.4 fusion.6
  17.7 2.0 collective-permute-start.5
  19.8 2.0 collective-permute-start.3
  21.8 245.0 %gather.1 = (bf16[1280,5120]{1,0:T(8,128)(2,1)}, bf16[5120,1280]{1,0:T(8,128)(2,1)}, bf16[2048,640]{1,0:T(8,128)(2,1)}) custom-call(bf16[320,2560]{1,0:T(8,128)(2,1)} %w1_ref.1, bf16[1280,640]{1,0:T(8,128)(2,1)} %w2_ref.1, bf16[4096,640]{1,0:T(8,128)(2,1)} %xo_ref.7), custom_call_target="tpu_custom_call" | custom-call | bytes 300000000 | tf_op jit(solution)/shard_map/gather/pallas_call | solution.py:144
  266.8 27.7 %up.4 = (bf16[4096,5120]{1,0:T(8,128)(2,1)}, f32[4096,5120]{1,0:T(8,128)}) custom-call(bf16[4096,640]{1,0:T(8,128)(2,1)} %xo_ref.7, bf16[2048,640]{1,0:T(8,128)(2,1)} %get-tuple-element.20.xt_ref, bf16[1280,5120]{1,0:T(8,128)(2,1)} %get-tuple-element.19.w_ref), custom_call_target="tpu_custom_call" | custom-call | flops 13421772800 | bytes 44564480 | tf_op jit(solution)/shard_map/up/pallas_call | solution.py:197
  294.5 27.7 %up.5 = (bf16[4096,5120]{1,0:T(8,128)(2,1)}, f32[4096,5120]{1,0:T(8,128)}) custom-call(bf16[4096,640]{1,0:T(8,128)(2,1)} %xo_ref.7, bf16[2048,640]{1,0:T(8,128)(2,1)} %get-tuple-element.20.xt_ref, bf16[1280,5120]{1,0:T(8,128)(2,1)} %get-tuple-element.19.w_ref, ...), custom_call_target="tpu_custom_call", output_to_operand_aliasing={{0}: (3, {}), {1}: (4, {})} | custom-call | flops 13421772800 | bytes 44564480 | tf_op jit(solution)/shard_map/up/pallas_call | solution.py:197
  322.3 0.6 add_add_fusion
  322.9 7.8 copy.25
  330.7 3.0 copy.24
  333.8 1.5 collective-permute-start.2
  335.3 2.4 copy.21.xt_ref
  337.7 27.7 %up.6 = (bf16[4096,5120]{1,0:T(8,128)(2,1)}, f32[4096,5120]{1,0:T(8,128)}) custom-call(bf16[4096,640]{1,0:T(8,128)(2,1)} %xo_ref.7, bf16[1024,640]{1,0:T(8,128)(2,1)} %copy.21.xt_ref, bf16[1280,5120]{1,0:T(8,128)(2,1)} %get-tuple-element.19.w_ref, bf16[4096,5120]{1,0:T(8,128)(2,1)} %get-tuple-element.23.rest_0_, ...), custom_call_target="tpu_custom_call", output_to_operand_aliasing={{0}: (3, {}), {1}: (4, {})} | custom-call | flops 13421772800 | bytes 44564480 | tf_op jit(solution)/shard_map/up/pallas_call | solution.py:197
  365.4 2.4 copy.22.xt_ref
  367.8 27.7 %up.7 = (bf16[4096,5120]{1,0:T(8,128)(2,1)}, f32[4096,5120]{1,0:T(8,128)}) custom-call(bf16[4096,640]{1,0:T(8,128)(2,1)} %xo_ref.7, bf16[1024,640]{1,0:T(8,128)(2,1)} %copy.22.xt_ref, bf16[1280,5120]{1,0:T(8,128)(2,1)} %get-tuple-element.19.w_ref, bf16[4096,5120]{1,0:T(8,128)(2,1)} %get-tuple-element.25.rest_0_, ...), custom_call_target="tpu_custom_call", output_to_operand_aliasing={{0}: (3, {}), {1}: (4, {})} | custom-call | flops 13421772800 | bytes 44564480 | tf_op jit(solution)/shard_map/up/pallas_call | solution.py:197
  395.5 19.8 %dw2.2.dep_ref = f32[640,2560]{1,0:T(8,128)} custom-call(s32[1]{0:T(128)} %bitcast.9.s_ref, bf16[640,4096]{1,0:T(8,128)(2,1)} %bitcast.15, bf16[4096,5120]{1,0:T(8,128)(2,1)} %get-tuple-element.27.a_ref, f32[4096,5120]{1,0:T(8,128)} %get-tuple-element.29.dep_ref.d_ref), custom_call_target="tpu_custom_call" | custom-call | flops 13421772800 | bytes 32768000 | tf_op jit(solution)/shard_map/dw2/pallas_call | solution.py:281
  415.3 3.9 constant_dynamic-slice_fusion
  419.3 21.0 %maximum_maximum_fusion.x_ref = bf16[1280,4096]{1,0:T(8,128)(2,1)} fusion(bf16[640,1024]{1,0:T(8,128)(2,1)} %bitcast.6, bf16[640,1024]{1,0:T(8,128)(2,1)} %bitcast.5, bf16[640,2048]{1,0:T(8,128)(2,1)S(1)} %bitcast.18, bf16[640,4096]{1,0:T(8,128)(2,1)} %bitcast.17), kind=kLoop, calls=%fused_computation | loop fusion | flops 41943040 | bytes 20971520 | tf_op jit(solution)/shard_map/concatenate | solution.py:373
  440.3 19.3 %dw2.3.rest_0_ = f32[640,2560]{1,0:T(8,128)} custom-call(s32[1]{0:T(128)} %bitcast.7.s_ref, bf16[640,4096]{1,0:T(8,128)(2,1)} %bitcast.16, bf16[4096,5120]{1,0:T(8,128)(2,1)} %get-tuple-element.27.a_ref, f32[640,2560]{1,0:T(8,128)} %dw2.2.dep_ref), custom_call_target="tpu_custom_call" | custom-call | flops 13421772800 | bytes 32768000 | tf_op jit(solution)/shard_map/dw2/pallas_call | solution.py:281
  459.6 23.5 %du.4.rest_0_ = bf16[4096,5120]{1,0:T(8,128)(2,1)} custom-call(bf16[4096,640]{1,0:T(8,128)(2,1)} %go_ref.7, bf16[1024,640]{1,0:T(8,128)(2,1)} %collective-permute-done.5.gt_ref, bf16[5120,1280]{1,0:T(8,128)(2,1)} %get-tuple-element.28.w_ref, f32[4096,5120]{1,0:T(8,128)} %get-tuple-element.29.dep_ref.d_ref, f32[640,2560]{1,0:T(8,128)} %dw2.3.rest_0_), custom_call_target="tpu_custom_call" | custom-call | flops 13421772800 | bytes 44564480 | tf_op jit(solution)/shard_map/du/pallas_call | solution.py:237
  483.1 23.5 %du.5.rest_0_ = bf16[4096,5120]{1,0:T(8,128)(2,1)} custom-call(bf16[4096,640]{1,0:T(8,128)(2,1)} %go_ref.7, bf16[1024,640]{1,0:T(8,128)(2,1)} %collective-permute-done.4.gt_ref, bf16[5120,1280]{1,0:T(8,128)(2,1)} %get-tuple-element.28.w_ref, f32[4096,5120]{1,0:T(8,128)} %get-tuple-element.29.dep_ref.d_ref, ...), custom_call_target="tpu_custom_call", output_to_operand_aliasing={{}: (4, {})} | custom-call | flops 13421772800 | bytes 44564480 | tf_op jit(solution)/shard_map/du/pallas_call | solution.py:237
  506.6 23.5 %du.6.rest_0_ = bf16[4096,5120]{1,0:T(8,128)(2,1)} custom-call(bf16[4096,640]{1,0:T(8,128)(2,1)} %go_ref.7, bf16[1024,640]{1,0:T(8,128)(2,1)} %collective-permute-done.3.gt_ref, bf16[5120,1280]{1,0:T(8,128)(2,1)} %get-tuple-element.28.w_ref, f32[4096,5120]{1,0:T(8,128)} %get-tuple-element.29.dep_ref.d_ref, ...), custom_call_target="tpu_custom_call", output_to_operand_aliasing={{}: (4, {})} | custom-call | flops 13421772800 | bytes 44564480 | tf_op jit(solution)/shard_map/du/pallas_call | solution.py:237
  530.1 23.4 %du.7.u_ref.dep_ref = bf16[4096,5120]{1,0:T(8,128)(2,1)} custom-call(bf16[4096,640]{1,0:T(8,128)(2,1)} %go_ref.7, bf16[1024,640]{1,0:T(8,128)(2,1)} %collective-permute-done.2.gt_ref, bf16[5120,1280]{1,0:T(8,128)(2,1)} %get-tuple-element.28.w_ref, f32[4096,5120]{1,0:T(8,128)} %get-tuple-element.29.dep_ref.d_ref, ...), custom_call_target="tpu_custom_call", output_to_operand_aliasing={{}: (4, {})} | custom-call | flops 13421772800 | bytes 44564480 | tf_op jit(solution)/shard_map/du/pallas_call | solution.py:237
  553.6 20.4 %dw1.2 = (f32[320,2560]{1,0:T(8,128)}, f32[320,2560]{1,0:T(8,128)}) custom-call(s32[3]{0:T(128)} %get-tuple-element.57.s_ref, bf16[1280,4096]{1,0:T(8,128)(2,1)} %maximum_maximum_fusion.x_ref, bf16[4096,5120]{1,0:T(8,128)(2,1)} %du.7.u_ref.dep_ref, bf16[4096,5120]{1,0:T(8,128)(2,1)} %du.7.u_ref.dep_ref), custom_call_target="tpu_custom_call" | custom-call | flops 13421772800 | bytes 32768000 | tf_op jit(solution)/shard_map/dw1/pallas_call | solution.py:320
  574.0 0.5 collective-permute-start.7
  574.5 20.3 %dw1.3 = (f32[320,2560]{1,0:T(8,128)}, f32[320,2560]{1,0:T(8,128)}) custom-call(s32[3]{0:T(128)} %get-tuple-element.56.s_ref, bf16[1280,4096]{1,0:T(8,128)(2,1)} %maximum_maximum_fusion.x_ref, bf16[4096,5120]{1,0:T(8,128)(2,1)} %du.7.u_ref.dep_ref, f32[320,2560]{1,0:T(8,128)} %get-tuple-element.30.dep_ref), custom_call_target="tpu_custom_call" | custom-call | flops 13421772800 | bytes 32768000 | tf_op jit(solution)/shard_map/dw1/pallas_call | solution.py:320
  595.0 3.8 constant_dynamic-slice_fusion.1
  599.1 22.3 %shard_map.75.dep_ref = bf16[4096,640]{1,0:T(8,128)(2,1)} custom-call(bf16[4096,5120]{1,0:T(8,128)(2,1)} %get-tuple-element.27.a_ref, bf16[5120,1280]{1,0:T(8,128)(2,1)} %get-tuple-element.28.w_ref, f32[320,2560]{1,0:T(8,128)} %get-tuple-element.31.dep_ref), custom_call_target="tpu_custom_call" | custom-call | flops 13421772800 | bytes 27525120 | tf_op jit(solution)/shard_map/pallas_call | solution.py:262
  621.5 3.8 slice_add_fusion.10
  625.2 1.5 collective-permute-start.10
  626.7 0.5 collective-permute-start.12
  627.3 1.5 collective-permute-start.14
  628.8 0.5 collective-permute-start.8
  629.3 22.2 %shard_map.76.dep_ref = bf16[4096,640]{1,0:T(8,128)(2,1)} custom-call(bf16[4096,5120]{1,0:T(8,128)(2,1)} %get-tuple-element.27.a_ref, bf16[5120,1280]{1,0:T(8,128)(2,1)} %get-tuple-element.28.w_ref, bf16[4096,640]{1,0:T(8,128)(2,1)} %shard_map.75.dep_ref), custom_call_target="tpu_custom_call", output_to_operand_aliasing={{}: (2, {})} | custom-call | flops 13421772800 | bytes 27525120 | tf_op jit(solution)/shard_map/pallas_call | solution.py:262
  651.5 4.6 slice_add_fusion.2
  656.1 0.9 copy-done.4
  657.0 1.5 collective-permute-start.18
  658.5 5.6 collective-permute-done.12
  664.1 1.5 collective-permute-start.20
  665.6 16.1 %collective-permute-done.14 = f32[320,640]{1,0:T(8,128)} collective-permute-done((f32[320,640]{1,0:T(8,128)}, f32[320,640]{1,0:T(8,128)}, u32[]{:S(2)}, u32[]{:S(2)}) %collective-permute-start.14) | collective-permute-done | bytes 819232 | tf_op jit(solution)/shard_map/ppermute | solution.py:350
  681.8 17.6 %collective-permute-done.8 = f32[320,640]{1,0:T(8,128)} collective-permute-done((f32[320,640]{1,0:T(8,128)}, f32[320,640]{1,0:T(8,128)}, u32[]{:S(2)}, u32[]{:S(2)}) %collective-permute-start.8) | collective-permute-done | bytes 819232 | tf_op jit(solution)/shard_map/ppermute | solution.py:350
  699.3 4.7 fusion.5
  704.5 22.5 %shard_map.77.dep_ref = bf16[4096,640]{1,0:T(8,128)(2,1)} custom-call(bf16[4096,5120]{1,0:T(8,128)(2,1)} %du.7.u_ref.dep_ref, bf16[1280,5120]{1,0:T(8,128)(2,1)} %get-tuple-element.19.w_ref, bf16[4096,640]{1,0:T(8,128)(2,1)} %shard_map.76.dep_ref), custom_call_target="tpu_custom_call" | custom-call | flops 13421772800 | bytes 27525120 | tf_op jit(solution)/shard_map/pallas_call | solution.py:262
  727.0 1.6 collective-permute-start.11
  728.6 0.5 collective-permute-start.13
  729.1 5.2 collective-permute-done.18
  734.8 0.7 copy-done.3
  735.5 33.3 %collective-permute-done.20 = f32[320,1280]{1,0:T(8,128)} collective-permute-done((f32[320,1280]{1,0:T(8,128)S(1)}, f32[320,1280]{1,0:T(8,128)}, u32[]{:S(2)}, u32[]{:S(2)}) %collective-permute-start.20) | collective-permute-done | bytes 1638432 | tf_op jit(solution)/shard_map/ppermute | solution.py:350
  768.7 4.4 fusion.1
  773.2 0.5 collective-permute-start.19
  773.7 1.6 collective-permute-start.21
  775.3 22.3 %shard_map.78 = bf16[4096,640]{1,0:T(8,128)(2,1)} custom-call(bf16[4096,5120]{1,0:T(8,128)(2,1)} %du.7.u_ref.dep_ref, bf16[1280,5120]{1,0:T(8,128)(2,1)} %get-tuple-element.19.w_ref, bf16[4096,640]{1,0:T(8,128)(2,1)} %shard_map.77.dep_ref), custom_call_target="tpu_custom_call", output_to_operand_aliasing={{}: (2, {})} | custom-call | flops 13421772800 | bytes 27525120 | tf_op jit(solution)/shard_map/pallas_call | solution.py:262
  797.6 1.5 add.107
  799.1 1.5 add.111
  800.6 1.5 add.115
  802.1 1.2 add.119
  803.3 2.1 pad_maximum_fusion
  805.4 13.3 %collective-permute-done.19 = f32[320,1280]{1,0:T(8,128)} collective-permute-done((f32[320,1280]{1,0:T(8,128)S(1)}, f32[320,1280]{1,0:T(8,128)}, u32[]{:S(2)}, u32[]{:S(2)}) %collective-permute-start.19) | collective-permute-done | bytes 1638432 | tf_op jit(solution)/shard_map/ppermute | solution.py:356
  818.7 1.6 add_bitcast_fusion.1
  820.3 30.7 %collective-permute-done.21 = f32[320,1280]{1,0:T(8,128)} collective-permute-done((f32[320,1280]{1,0:T(8,128)S(1)}, f32[320,1280]{1,0:T(8,128)}, u32[]{:S(2)}, u32[]{:S(2)}) %collective-permute-start.21) | collective-permute-done | bytes 1638432 | tf_op jit(solution)/shard_map/ppermute | solution.py:356
  851.0 1.6 add_bitcast_fusion
  852.9 3.1 copy.26
  (33 shorter events, 1.9 us)
Async XLA Ops:
  8.5 6.9 copy-start
  12.1 321.7 %collective-permute-start.1 = (bf16[1024,640]{0,1:T(8,128)(2,1)}, bf16[1024,640]{0,1:T(8,128)(2,1)}, u32[]{:S(2)}, u32[]{:S(2)}) collective-permute-start(bf16[1024,640]{0,1:T(8,128)(2,1)} %get-tuple-element.54), channel_id=1, source_target_pairs={{0,4},{4,0},{1,5},{5,1},{2,6},{6,2},{3,7},{7,3},{8,12},{12,8},{9,1... | collective-permute-start | bytes 3932168 | tf_op jit(solution)/shard_map/ppermute | solution.py:353
  15.3 350.1 %collective-permute-start = (bf16[1024,640]{0,1:T(8,128)(2,1)}, bf16[1024,640]{0,1:T(8,128)(2,1)}, u32[]{:S(2)}, u32[]{:S(2)}) collective-permute-start(bf16[1024,640]{0,1:T(8,128)(2,1)} %get-tuple-element.55), channel_id=1, source_target_pairs={{0,4},{4,0},{1,5},{5,1},{2,6},{6,2},{3,7},{7,3},{8,12},{12,8},{9,1... | collective-permute-start | bytes 3932168 | tf_op jit(solution)/shard_map/ppermute | solution.py:353
  17.7 441.9 %collective-permute-start.5 = (bf16[1024,640]{1,0:T(8,128)(2,1)}, bf16[1024,640]{1,0:T(8,128)(2,1)}, u32[]{:S(2)}, u32[]{:S(2)}) collective-permute-start(bf16[1024,640]{1,0:T(8,128)(2,1)} %get-tuple-element.50), channel_id=1, source_target_pairs={{0,4},{4,0},{1,5},{5,1},{2,6},{6,2},{3,7},{7,3},{8,12},{12,8},{9,1... | collective-permute-start | bytes 3932168 | tf_op jit(solution)/shard_map/ppermute | solution.py:353
  19.7 463.4 %collective-permute-start.4 = (bf16[1024,640]{1,0:T(8,128)(2,1)}, bf16[1024,640]{1,0:T(8,128)(2,1)}, u32[]{:S(2)}, u32[]{:S(2)}) collective-permute-start(bf16[1024,640]{1,0:T(8,128)(2,1)} %get-tuple-element.51), channel_id=1, source_target_pairs={{0,4},{4,0},{1,5},{5,1},{2,6},{6,2},{3,7},{7,3},{8,12},{12,8},{9,1... | collective-permute-start | bytes 3932168 | tf_op jit(solution)/shard_map/ppermute | solution.py:353
  19.8 486.8 %collective-permute-start.3 = (bf16[1024,640]{1,0:T(8,128)(2,1)}, bf16[1024,640]{1,0:T(8,128)(2,1)}, u32[]{:S(2)}, u32[]{:S(2)}) collective-permute-start(bf16[1024,640]{1,0:T(8,128)(2,1)} %get-tuple-element.52), channel_id=1, source_target_pairs={{0,4},{4,0},{1,5},{5,1},{2,6},{6,2},{3,7},{7,3},{8,12},{12,8},{9,1... | collective-permute-start | bytes 3932168 | tf_op jit(solution)/shard_map/ppermute | solution.py:353
  333.8 196.4 %collective-permute-start.2 = (bf16[1024,640]{1,0:T(8,128)(2,1)}, bf16[1024,640]{1,0:T(8,128)(2,1)}, u32[]{:S(2)}, u32[]{:S(2)}) collective-permute-start(bf16[1024,640]{1,0:T(8,128)(2,1)} %get-tuple-element.53), channel_id=1, source_target_pairs={{0,4},{4,0},{1,5},{5,1},{2,6},{6,2},{3,7},{7,3},{8,12},{12,8},{9,1... | collective-permute-start | bytes 3932168 | tf_op jit(solution)/shard_map/ppermute | solution.py:353
  419.2 208.1 %collective-permute-start.17 = (f32[640,1280]{1,0:T(8,128)}, f32[640,1280]{1,0:T(8,128)}, u32[]{:S(2)}, u32[]{:S(2)}) collective-permute-start(f32[640,1280]{1,0:T(8,128)} %constant_dynamic-slice_fusion), channel_id=1, source_target_pairs={{0,1},{1,0},{2,3},{3,2},{4,5},{5,4},{6,7},{7,6},{8,9},{9,8},{10,11... | collective-permute-start | bytes 9830408 | tf_op jit(solution)/shard_map/ppermute | solution.py:347
  574.0 47.4 %collective-permute-start.7 = (f32[320,2560]{1,0:T(8,128)}, f32[320,2560]{1,0:T(8,128)}, u32[]{:S(2)}, u32[]{:S(2)}) collective-permute-start(f32[320,2560]{1,0:T(8,128)} %get-tuple-element.33), channel_id=1, source_target_pairs={{0,1},{1,0},{2,3},{3,2},{4,5},{5,4},{6,7},{7,6},{8,9},{9,8},{10,11... | collective-permute-start | bytes 9830408 | tf_op jit(solution)/shard_map/ppermute | solution.py:347
  594.8 34.0 %collective-permute-start.6 = (f32[320,2560]{1,0:T(8,128)}, f32[320,2560]{1,0:T(8,128)}, u32[]{:S(2)}, u32[]{:S(2)}) collective-permute-start(f32[320,2560]{1,0:T(8,128)} %get-tuple-element.32), channel_id=1, source_target_pairs={{0,1},{1,0},{2,3},{3,2},{4,5},{5,4},{6,7},{7,6},{8,9},{9,8},{10,11... | collective-permute-start | bytes 9830408 | tf_op jit(solution)/shard_map/ppermute | solution.py:347
  598.8 129.8 %collective-permute-start.16 = (f32[640,1280]{1,0:T(8,128)}, f32[640,1280]{1,0:T(8,128)}, u32[]{:S(2)}, u32[]{:S(2)}) collective-permute-start(f32[640,1280]{1,0:T(8,128)} %constant_dynamic-slice_fusion.1), channel_id=1, source_target_pairs={{0,1},{1,0},{2,3},{3,2},{4,5},{5,4},{6,7},{7,6},{8,9},{9,8},{10,11... | collective-permute-start | bytes 9830408 | tf_op jit(solution)/shard_map/ppermute | solution.py:347
  599.1 22.3 %copy-start.1 = (f32[320,2560]{1,0:T(8,128)S(1)}, f32[320,2560]{1,0:T(8,128)}, u32[]{:S(2)}) copy-start(f32[320,2560]{1,0:T(8,128)} %get-tuple-element.30.dep_ref) | copy-start | bytes 9830404
  625.2 30.9 %collective-permute-start.10 = (f32[320,640]{1,0:T(8,128)}, f32[320,640]{1,0:T(8,128)S(1)}, u32[]{:S(2)}, u32[]{:S(2)}) collective-permute-start(f32[320,640]{1,0:T(8,128)} %get-tuple-element.49), channel_id=1, source_target_pairs={{0,2},{1,3},{2,0},{3,1},{4,6},{5,7},{6,4},{7,5},{8,10},{9,11},{10,... | collective-permute-start | bytes 2457608 | tf_op jit(solution)/shard_map/ppermute | solution.py:350
  626.7 37.4 %collective-permute-start.12 = (f32[320,640]{1,0:T(8,128)}, f32[320,640]{1,0:T(8,128)S(1)}, u32[]{:S(2)}, u32[]{:S(2)}) collective-permute-start(f32[320,640]{1,0:T(8,128)} %get-tuple-element.48), channel_id=1, source_target_pairs={{0,2},{1,3},{2,0},{3,1},{4,6},{5,7},{6,4},{7,5},{8,10},{9,11},{10,... | collective-permute-start | bytes 2457608 | tf_op jit(solution)/shard_map/ppermute | solution.py:350
  627.3 54.5 %collective-permute-start.14 = (f32[320,640]{1,0:T(8,128)}, f32[320,640]{1,0:T(8,128)}, u32[]{:S(2)}, u32[]{:S(2)}) collective-permute-start(f32[320,640]{1,0:T(8,128)} %get-tuple-element.47), channel_id=1, source_target_pairs={{0,2},{1,3},{2,0},{3,1},{4,6},{5,7},{6,4},{7,5},{8,10},{9,11},{10,... | collective-permute-start | bytes 2457608 | tf_op jit(solution)/shard_map/ppermute | solution.py:350
  628.8 70.5 %collective-permute-start.8 = (f32[320,640]{1,0:T(8,128)}, f32[320,640]{1,0:T(8,128)}, u32[]{:S(2)}, u32[]{:S(2)}) collective-permute-start(f32[320,640]{1,0:T(8,128)} %get-tuple-element.46), channel_id=1, source_target_pairs={{0,2},{1,3},{2,0},{3,1},{4,6},{5,7},{6,4},{7,5},{8,10},{9,11},{10,... | collective-permute-start | bytes 2457608 | tf_op jit(solution)/shard_map/ppermute | solution.py:350
  651.5 47.8 %copy-start.2 = (f32[320,2560]{1,0:T(8,128)S(1)}, f32[320,2560]{1,0:T(8,128)}, u32[]{:S(2)}) copy-start(f32[320,2560]{1,0:T(8,128)} %get-tuple-element.31.dep_ref) | copy-start | bytes 9830404
  656.1 0.9 copy-start.4
  657.0 77.3 %collective-permute-start.18 = (f32[320,1280]{1,0:T(8,128)}, f32[320,1280]{1,0:T(8,128)S(1)}, u32[]{:S(2)}, u32[]{:S(2)}) collective-permute-start(f32[320,1280]{1,0:T(8,128)} %get-tuple-element.40), channel_id=1, source_target_pairs={{0,2},{1,3},{2,0},{3,1},{4,6},{5,7},{6,4},{7,5},{8,10},{9,11},{10,... | collective-permute-start | bytes 4915208 | tf_op jit(solution)/shard_map/ppermute | solution.py:350
  664.1 17.7 %copy-start.5 = (f32[320,640]{1,0:T(8,128)}, f32[320,640]{1,0:T(8,128)S(1)}, u32[]{:S(2)}) copy-start(f32[320,640]{1,0:T(8,128)S(1)} %collective-permute-done.12) | copy-start | bytes 2457604
  664.1 104.6 %collective-permute-start.20 = (f32[320,1280]{1,0:T(8,128)S(1)}, f32[320,1280]{1,0:T(8,128)}, u32[]{:S(2)}, u32[]{:S(2)}) collective-permute-start(f32[320,1280]{1,0:T(8,128)S(1)} %get-tuple-element.41), channel_id=1, source_target_pairs={{0,2},{1,3},{2,0},{3,1},{4,6},{5,7},{6,4},{7,5},{8,10},{9,11},{10,... | collective-permute-start | bytes 4915208 | tf_op jit(solution)/shard_map/ppermute | solution.py:350
  704.1 69.6 %collective-permute-start.9 = (f32[320,640]{1,0:T(8,128)}, f32[320,640]{1,0:T(8,128)}, u32[]{:S(2)}, u32[]{:S(2)}) collective-permute-start(f32[320,640]{1,0:T(8,128)} %get-tuple-element.42), channel_id=1, source_target_pairs={{0,8},{8,0},{1,9},{9,1},{2,10},{10,2},{3,11},{11,3},{4,12},{12,4},... | collective-permute-start | bytes 2457608 | tf_op jit(solution)/shard_map/ppermute | solution.py:356
  727.0 72.0 %collective-permute-start.11 = (f32[320,640]{1,0:T(8,128)}, f32[320,640]{1,0:T(8,128)}, u32[]{:S(2)}, u32[]{:S(2)}) collective-permute-start(f32[320,640]{1,0:T(8,128)} %get-tuple-element.45), channel_id=1, source_target_pairs={{0,8},{8,0},{1,9},{9,1},{2,10},{10,2},{3,11},{11,3},{4,12},{12,4},... | collective-permute-start | bytes 2457608 | tf_op jit(solution)/shard_map/ppermute | solution.py:356
  728.6 71.9 %collective-permute-start.13 = (f32[320,640]{1,0:T(8,128)}, f32[320,640]{1,0:T(8,128)}, u32[]{:S(2)}, u32[]{:S(2)}) collective-permute-start(f32[320,640]{1,0:T(8,128)} %get-tuple-element.44), channel_id=1, source_target_pairs={{0,8},{8,0},{1,9},{9,1},{2,10},{10,2},{3,11},{11,3},{4,12},{12,4},... | collective-permute-start | bytes 2457608 | tf_op jit(solution)/shard_map/ppermute | solution.py:356
  734.3 1.2 copy-start.3
  734.3 67.7 %collective-permute-start.15 = (f32[320,640]{1,0:T(8,128)S(1)}, f32[320,640]{1,0:T(8,128)}, u32[]{:S(2)}, u32[]{:S(2)}) collective-permute-start(f32[320,640]{1,0:T(8,128)S(1)} %get-tuple-element.43), channel_id=1, source_target_pairs={{0,8},{8,0},{1,9},{9,1},{2,10},{10,2},{3,11},{11,3},{4,12},{12,4},... | collective-permute-start | bytes 2457608 | tf_op jit(solution)/shard_map/ppermute | solution.py:356
  773.2 45.5 %collective-permute-start.19 = (f32[320,1280]{1,0:T(8,128)S(1)}, f32[320,1280]{1,0:T(8,128)}, u32[]{:S(2)}, u32[]{:S(2)}) collective-permute-start(f32[320,1280]{1,0:T(8,128)S(1)} %get-tuple-element.38), channel_id=1, source_target_pairs={{0,8},{8,0},{1,9},{9,1},{2,10},{10,2},{3,11},{11,3},{4,12},{12,4},... | collective-permute-start | bytes 4915208 | tf_op jit(solution)/shard_map/ppermute | solution.py:356
  773.7 77.4 %collective-permute-start.21 = (f32[320,1280]{1,0:T(8,128)S(1)}, f32[320,1280]{1,0:T(8,128)}, u32[]{:S(2)}, u32[]{:S(2)}) collective-permute-start(f32[320,1280]{1,0:T(8,128)S(1)} %get-tuple-element.39), channel_id=1, source_target_pairs={{0,8},{8,0},{1,9},{9,1},{2,10},{10,2},{3,11},{11,3},{4,12},{12,4},... | collective-permute-start | bytes 4915208 | tf_op jit(solution)/shard_map/ppermute | solution.py:356
